TPU v7x, 256 devices: a whole 4x4x8 slice. The times are simulated.
256 devices in a mesh: win: 16 (over x, y), dof: 16 (over z, core).
Axes of the slice: x: 4, y: 4, z: 8, core: 2. Of those that a mesh axis runs over, the one named last changes fastest.
Arguments:
- snapshots: bfloat16 [524288, 1024], P('dof', 'win'), may hold values from -6 to 6
- sketch_matrix: bfloat16 [524288, 128], P('dof'), may hold values from -0.0078125 to 0.0078125
- pivots: int32 [32, 64], P('win'), may hold values from 0 to 127
Outputs:
- singular: float32 [32, 64], P('win')
- projections: float32 [32, 64, 32], P('win')
All inputs are finite; a program needn't handle non-finite values.
Results may differ from a plain program's by a relative error of at most 0.0003.
Values sent between devices are 32-bit elements; how exact they have to be, the bound alone decides.
A program may use at most 64 MiB of HBM per device.

v0:
```python
import math

import jax
import jax.numpy as jnp
from jax import lax
from jax.sharding import PartitionSpec as P

RANK = 64
ORTH_ITERS = 2


HIGHEST_PREC = lax.Precision.HIGHEST


def total_of_pieces(shard, axis):
    return lax.all_gather(shard, axis).sum(0)


def sent_to_all(shard, axis):
    peers = lax.axis_size(axis)
    return lax.all_to_all(
        jnp.broadcast_to(shard[None], (peers, *shard.shape)), axis, 0, 0, tiled=True
    )


def joined_along(parts, dim):
    parts = jnp.moveaxis(parts, 0, dim)
    lengths = parts.shape
    return parts.reshape(*lengths[:dim], lengths[dim] * lengths[dim + 1], *lengths[dim + 2 :])


def collect(shard, axis, dim):
    parts = sent_to_all(shard, axis)
    return joined_along(parts, dim)


def orthogonal(prefix_grams):
    batch_count = prefix_grams.shape[0]
    sketch_width = prefix_grams.shape[1]
    basis_cols = jnp.broadcast_to(
        jnp.eye(sketch_width, RANK, dtype=jnp.float32), (batch_count, sketch_width, RANK)
    )
    for sweep_index in range(ORTH_ITERS):
        images = jnp.einsum("wij,wjk->wik", prefix_grams, basis_cols, precision=HIGHEST_PREC)
        inner_gram = jnp.einsum("wik,wil->wkl", images, images, precision=HIGHEST_PREC)
        chol_factor = jnp.linalg.cholesky(inner_gram)
        solved = jax.scipy.linalg.solve_triangular(
            chol_factor, jnp.swapaxes(images, 1, 2), lower=True
        )
        basis_cols = jnp.swapaxes(solved, 1, 2)
    return basis_cols


def finish(prefix_grams, basis_cols, window_blocks, pivots):
    images = jnp.einsum("wij,wjk->wik", prefix_grams, basis_cols, precision=HIGHEST_PREC)
    singular = jnp.sqrt(jnp.sum(basis_cols * images, axis=1))
    sketch_width = basis_cols.shape[1]
    pivot_table = (
        pivots[:, :, None] == jnp.arange(sketch_width, dtype=jnp.int32)[None, None, :]
    ).astype(jnp.float32)
    pivot_weight = jnp.einsum(
        "wrk,wkr->wr", pivot_table, basis_cols, precision=HIGHEST_PREC
    ) * math.sqrt(sketch_width)
    projections = (
        jnp.einsum("wkr,wks->wrs", basis_cols, window_blocks, precision=HIGHEST_PREC)
        * pivot_weight[:, :, None]
    )
    return (singular, projections)


def masked_gram(gathered, limit):
    column_ids = lax.iota(jnp.int32, gathered.shape[1])
    keep_mask = (column_ids < limit).astype(jnp.float32)
    return jnp.dot(gathered * keep_mask[None, :], gathered.T, precision=HIGHEST_PREC)


def local(snapshots, sketch_matrix, pivots):
    windows_here = pivots.shape[0]
    sketch_width = sketch_matrix.shape[1]
    local_cols = snapshots.shape[1]
    snap_count = local_cols // windows_here
    win_position = lax.axis_index("win")
    partial_value = lax.dot_general(
        sketch_matrix, snapshots, (((0,), (0,)), ((), ())), preferred_element_type=jnp.float32
    )
    coefficients = total_of_pieces(partial_value, "dof")
    window_blocks = jnp.transpose(
        coefficients.reshape(sketch_width, windows_here, snap_count), (1, 0, 2)
    )
    window_grams = jnp.einsum("wks,wjs->wkj", window_blocks, window_blocks, precision=HIGHEST_PREC)
    own_prefix = jnp.cumsum(window_grams, axis=0)
    gathered = collect(coefficients, "win", 1)
    earlier = masked_gram(gathered, win_position * local_cols)
    window_ids = win_position * windows_here + jnp.arange(windows_here, dtype=jnp.int32)
    snap_totals = (snap_count * (window_ids + 1)).astype(jnp.float32)
    identity = jnp.eye(sketch_width, dtype=jnp.float32)
    prefix_grams = identity[None] + (earlier[None] + own_prefix) / snap_totals[:, None, None]
    basis_cols = orthogonal(prefix_grams)
    singular, projections = finish(prefix_grams, basis_cols, window_blocks, pivots)
    return (singular, projections)


def solution(mesh):
    placed = (P("dof", "win"), P("dof", None), P("win", None))
    return jax.shard_map(
        local,
        mesh=mesh,
        in_specs=placed,
        out_specs=(P("win", None), P("win", None, None)),
        check_vma=False,
    )
```

profile of v0, /device:TPU:1, one launch (start us, length us, event | category | flops | bytes accessed | tf_op | source)
XLA Modules:
  0.0 96.5 jit_solution(2712634917362555724)
XLA Ops:
  0.6 0.0 copy-start
  0.6 6.2 %fusion.23 = f32[128,64]{0,1:T(8,128)S(1)} fusion(bf16[32768,64]{0,1:T(8,128)(2,1)} %param.6, bf16[32768,128]{1,0:T(8,128)(2,1)} %param.7), kind=kOutput, calls=%fused_computation.45 | convolution fusion | flops 536870912 | bytes 12615680 | tf_op jit(solution)/shard_map/dot_general | solution.py:83
  6.9 22.7 %all-gather = f32[2048,64]{0,1:T(8,128)S(1)} all-gather(f32[128,64]{0,1:T(8,128)S(1)} %fusion.23), channel_id=2, replica_groups=mesh['win'=16,'dof'=16] {'dof'}, dimensions={0}, use_global_device_ids=true | all-gather | bytes 557056 | tf_op jit(solution)/shard_map/all_gather | solution.py:16
  29.6 0.1 copy.17
  29.7 0.1 bitcast_reduce_fusion
  29.8 0.8 broadcast_in_dim.6
  30.7 6.8 %all-to-all-start = ((f32[16,128,64]{1,2,0:T(8,128)}), f32[16,128,64]{1,2,0:T(8,128)S(1)}, u32[]{:S(2)}, u32[]{:S(2)}) async-start(f32[16,128,64]{1,2,0:T(8,128)} %broadcast_in_dim.6), calls=%async_computation | async-start | bytes 1048576 | tf_op jit(solution)/shard_map/all_to_all | solution.py:21
  37.5 0.4 fusion.19
  37.9 9.7 %all-to-all-done = f32[16,128,64]{1,2,0:T(8,128)S(1)} async-done(((f32[16,128,64]{1,2,0:T(8,128)}), f32[16,128,64]{1,2,0:T(8,128)S(1)}, u32[]{:S(2)}, u32[]{:S(2)}) %all-to-all-start) | async-done | bytes 524320 | tf_op jit(solution)/shard_map/all_to_all | solution.py:21
  47.6 1.2 %convolution_bitcast_fusion = f32[128,128]{1,0:T(8,128)S(1)} fusion(f32[16,128,64]{1,2,0:T(8,128)S(1)} %all-to-all-done, f32[16,64]{1,0:T(8,128)S(1)} %fusion.18), kind=kOutput, calls=%fused_computation.3 | convolution fusion | flops 201457664 | bytes 593920 | tf_op jit(solution)/shard_map/dot_general | solution.py:74
  48.8 0.1 fusion.1
  48.9 0.4 fusion.15
  49.2 0.2 fusion.20
  49.5 0.1 copy.8
  49.6 11.7 %custom-call.8 = f32[2,64,64]{2,1,0:T(8,128)S(1)} custom-call(f32[2,64,64]{2,1,0:T(8,128)S(1)} %fusion.13), custom_call_target="Cholesky" | custom-call | tf_op jit(solution)/shard_map/jit(cholesky)/cholesky | solution.py:46
  61.3 0.1 compare_reduce_fusion.1
  61.5 0.1 select_bitcast_fusion.1
  61.5 9.8 %custom-call.9 = f32[2,1,64,64]{2,3,1,0:T(8,128)S(1)} custom-call(f32[2,1,64,64]{3,2,1,0:T(8,128)S(1)} %select_bitcast_fusion.1), custom_call_target="InvertDiagBlocksLowerTriangular" | custom-call | tf_op jit(solution)/shard_map/jit(_solve_triangular)/vmap()/triangular_solve | solution.py:47
  71.4 0.3 fusion.10
  71.7 0.4 fusion.21
  72.0 0.2 fusion.22
  72.3 0.1 copy.9
  72.4 11.7 %custom-call.10 = f32[2,64,64]{2,1,0:T(8,128)S(1)} custom-call(f32[2,64,64]{2,1,0:T(8,128)S(1)} %fusion.9), custom_call_target="Cholesky" | custom-call | tf_op jit(solution)/shard_map/jit(cholesky)/cholesky | solution.py:46
  84.2 0.1 compare_reduce_fusion
  84.3 0.1 select_bitcast_fusion
  84.4 9.8 %custom-call.11 = f32[2,1,64,64]{2,3,1,0:T(8,128)S(1)} custom-call(f32[2,1,64,64]{3,2,1,0:T(8,128)S(1)} %select_bitcast_fusion), custom_call_target="InvertDiagBlocksLowerTriangular" | custom-call | tf_op jit(solution)/shard_map/jit(_solve_triangular)/vmap()/triangular_solve | solution.py:47
  94.2 0.0 copy-done
  94.2 0.4 select_reduce_fusion
  94.6 0.5 fusion.2
  95.0 0.8 convolution_multiply_fusion.1
  95.9 0.6 sqrt.3
  (11 shorter events, 0.1 us)
Async XLA Ops:
  0.6 93.6 %copy-start = (s32[2,64]{1,0:T(2,128)S(1)}, s32[2,64]{1,0:T(2,128)}, u32[]{:S(2)}) copy-start(s32[2,64]{1,0:T(2,128)} %param.8) | copy-start | bytes 1540
  30.7 16.9 %all-to-all-start = ((f32[16,128,64]{1,2,0:T(8,128)}), f32[16,128,64]{1,2,0:T(8,128)S(1)}, u32[]{:S(2)}, u32[]{:S(2)}) async-start(f32[16,128,64]{1,2,0:T(8,128)} %broadcast_in_dim.6), calls=%async_computation | async-start | bytes 1048576 | tf_op jit(solution)/shard_map/all_to_all | solution.py:21
where the time goes:
time: 96.7 us; the launch traced here: 96.5 us
  other arithmetic  43.8 us (45%)
  blocking collectives  22.7 us (23%)
  matrix products  10.9 us (11%)
  waiting for transfers between devices  9.68 us (10%)
  starting transfers between devices  6.75 us (7%)
  local copies, waits for them, and re-layouts  1.68 us (2%)
    another operation x7, other arithmetic, orthogonal(): chol_factor = jnp.linalg.cholesky(inner_gram)  23.8 us
    all_gather x1, blocking collectives, total_of_pieces(): return lax.all_gather(shard, axis).sum(0)  22.7 us
    another operation x5, other arithmetic, orthogonal(): jax.scipy.linalg.solve_triangular(chol_factor, jnp.swapaxes(images, 1, 2)...  19.8 us
    all_to_all x1, waiting for transfers between devices, sent_to_all(): lax.all_to_all(jnp.broadcast_to(shard[None], (peers, *shard.shape)), axis...  9.68 us
    all_to_all x1, starting transfers between devices, sent_to_all(): lax.all_to_all(jnp.broadcast_to(shard[None], (peers, *shard.shape)), axis...  6.75 us
    dot_general x1, matrix products, local(): lax.dot_general(sketch_matrix, snapshots, (((0,), (0,)), ((), ())), prefe...  6.24 us
  transfers between devices with their start and end apart: 1, of which 1 were waited for; matrix products, arithmetic and copies ran while one was open for 0% of the time, Pallas kernels for 0%

commit v1 on v0

v1 whole, which is shorter than its diff:
```python
import functools
import math

import jax
import jax.numpy as jnp
from jax import lax
from jax.experimental import pallas as pl
from jax.experimental.pallas import tpu as pltpu
from jax.sharding import PartitionSpec as P

HIGHEST_PREC = lax.Precision.HIGHEST
RANK = 64
NT = (((1,), (1,)), ((), ()))


def dot_nt(a, b):
    return lax.dot_general(a, b, NT, precision=HIGHEST_PREC, preferred_element_type=jnp.float32)


def dot_nn(a, b):
    return lax.dot_general(a, b, (((1,), (0,)), ((), ())), precision=HIGHEST_PREC, preferred_element_type=jnp.float32)


def halves(a, b):
    return jnp.concatenate([a[:, :64], b[:, :64]], axis=1), jnp.concatenate([a[:, 64:], b[:, 64:]], axis=1)


def split_rows(x):
    return [x[8 * i : 8 * i + 8, :] for i in range(8)]


def whiten(gram, low, high):
    lane = lax.broadcasted_iota(jnp.int32, (8, 128), 1)
    sub = lax.broadcasted_iota(jnp.int32, (8, 128), 0)
    base = lane - lane % 64
    v0, v1, v2 = split_rows(gram), split_rows(low), split_rows(high)
    for kb in range(8):
        cols = []
        for j in range(8):
            idx = base + (8 * kb + j)
            cols.append({i: jnp.take_along_axis(v0[i], idx, axis=1) for i in range(kb, 8)})
        diag = cols[0][kb]
        for p in range(8):
            pivot = jnp.broadcast_to(cols[p][kb][p : p + 1, :], (8, 128))
            if p:
                diag = jnp.where(sub >= p, pivot, diag)
            else:
                diag = pivot
            inv = 1.0 / pivot
            mult = {i: cols[p][i] * inv for i in range(kb, 8)}
            mult[kb] = jnp.where(sub > p, mult[kb], 0.0)
            for j in range(p + 1, 8):
                row = jnp.broadcast_to(cols[j][kb][p : p + 1, :], (8, 128))
                for i in range(kb, 8):
                    cols[j][i] = cols[j][i] - mult[i] * row
            for v in (v0, v1, v2) if kb < 7 else (v1, v2):
                row = jnp.broadcast_to(v[kb][p : p + 1, :], (8, 128))
                for i in range(kb, 8):
                    v[i] = v[i] - mult[i] * row
        scale = lax.rsqrt(diag)
        v1[kb] = v1[kb] * scale
        v2[kb] = v2[kb] * scale
    return jnp.concatenate(v1, axis=0), jnp.concatenate(v2, axis=0)


def masked_pair(low, high):
    first = lax.broadcasted_iota(jnp.int32, (64, 128), 1) < 64
    zero = jnp.zeros((64, 128), jnp.float32)
    top = jnp.concatenate([jnp.where(first, low, zero), jnp.where(first, high, zero)], axis=1)
    bottom = jnp.concatenate([jnp.where(first, zero, low), jnp.where(first, zero, high)], axis=1)
    return jnp.concatenate([top, bottom], axis=0)


def solve_windows(pa, pb, za, zb, pivots_row):
    alo, ahi = halves(pa, pb)
    zero = jnp.zeros((64, 64), jnp.float32)

    def block_rows(x, first):
        left = jnp.concatenate([x[:, :64], zero] if first else [zero, x[:, 64:]], axis=1)
        return left

    lo_a, lo_b = alo[:64], alo[64:]
    hi_a, hi_b = ahi[:64], ahi[64:]
    joint = jnp.concatenate(
        [
            jnp.concatenate([block_rows(lo_a, True), block_rows(hi_a, True)], axis=1),
            jnp.concatenate([block_rows(lo_a, False), block_rows(hi_a, False)], axis=1),
            jnp.concatenate([block_rows(lo_b, True), block_rows(hi_b, True)], axis=1),
            jnp.concatenate([block_rows(lo_b, False), block_rows(hi_b, False)], axis=1),
        ],
        axis=0,
    )
    low, high = lo_a, hi_a
    for sweep in range(2):
        if sweep:
            image = dot_nn(jnp.concatenate([low, high], axis=1), joint)
            low, high = image[:, :128], image[:, 128:]
        gram = dot_nt(jnp.concatenate([low, high], axis=1), masked_pair(low, high))
        low, high = whiten(gram, low, high)
    basis = jnp.concatenate([low, high], axis=1)
    image = dot_nn(basis, joint)
    prod = basis * image
    first = lax.broadcasted_iota(jnp.int32, (8, 256), 1) % 128 < 64
    row = lax.broadcasted_iota(jnp.int32, (8, 256), 0)
    pick = jnp.where((row == 0) & first, 1.0, 0.0) + jnp.where((row == 1) & (~first), 1.0, 0.0)
    squares = dot_nt(pick, prod)
    j = lax.broadcasted_iota(jnp.int32, (256, 128), 0)
    lane = lax.broadcasted_iota(jnp.int32, (256, 128), 1)
    own = (j // 64) % 2 == lane // 64
    dim = j % 64 + 64 * (j // 128)
    onehot = jnp.where(own & (dim == pivots_row), 1.0, 0.0)
    picked = dot_nn(basis, onehot)
    r = lax.broadcasted_iota(jnp.int32, (64, 128), 0)
    c = lax.broadcasted_iota(jnp.int32, (64, 128), 1)
    weight = jnp.sum(jnp.where(c % 64 == r, picked, 0.0), axis=0, keepdims=True) * math.sqrt(128)
    zlo, zhi = halves(za, zb)
    proj = dot_nt(jnp.concatenate([zlo, zhi], axis=1), masked_pair(low, high)) * weight
    return jnp.sqrt(squares[:2]), proj


def ortho_kernel(grams_ref, y_ref, pivots_ref, sing_ref, proj_ref):
    piv = pivots_ref[...]
    piv_row = jnp.concatenate([piv[0:1, :], piv[1:2, :]], axis=1)
    sing, proj = solve_windows(grams_ref[0], grams_ref[1], y_ref[:32, :], y_ref[32:, :], piv_row)
    sing_ref[...] = sing
    proj_ref[0] = proj[:, :64]
    proj_ref[1] = proj[:, 64:]


def ortho_call(grams, yt, pivots):
    sing, proj = pl.pallas_call(
        ortho_kernel,
        out_shape=(jax.ShapeDtypeStruct((2, 64), jnp.float32), jax.ShapeDtypeStruct((2, 32, 64), jnp.float32)),
        in_specs=[pl.BlockSpec(memory_space=pltpu.VMEM)] * 3,
        out_specs=(pl.BlockSpec(memory_space=pltpu.VMEM),) * 2,
    )(grams, yt, pivots)
    return sing, jnp.swapaxes(proj, 1, 2)


def total_of_pieces(shard, axis):
    return lax.all_gather(shard, axis).sum(0)


def sent_to_all(shard, axis):
    peers = lax.axis_size(axis)
    return lax.all_to_all(
        jnp.broadcast_to(shard[None], (peers, *shard.shape)), axis, 0, 0, tiled=True
    )


def joined_along(parts, dim):
    parts = jnp.moveaxis(parts, 0, dim)
    lengths = parts.shape
    return parts.reshape(*lengths[:dim], lengths[dim] * lengths[dim + 1], *lengths[dim + 2 :])


def collect(shard, axis, dim):
    parts = sent_to_all(shard, axis)
    return joined_along(parts, dim)


def masked_gram(gathered, limit):
    column_ids = lax.iota(jnp.int32, gathered.shape[1])
    keep_mask = (column_ids < limit).astype(jnp.float32)
    return jnp.dot(gathered * keep_mask[None, :], gathered.T, precision=HIGHEST_PREC)


def local(snapshots, sketch_matrix, pivots):
    windows_here = pivots.shape[0]
    sketch_width = sketch_matrix.shape[1]
    local_cols = snapshots.shape[1]
    snap_count = local_cols // windows_here
    win_position = lax.axis_index("win")
    partial_value = lax.dot_general(
        sketch_matrix, snapshots, (((0,), (0,)), ((), ())), preferred_element_type=jnp.float32
    )
    coefficients = total_of_pieces(partial_value, "dof")
    window_blocks = jnp.transpose(
        coefficients.reshape(sketch_width, windows_here, snap_count), (1, 0, 2)
    )
    window_grams = jnp.einsum("wks,wjs->wkj", window_blocks, window_blocks, precision=HIGHEST_PREC)
    own_prefix = jnp.cumsum(window_grams, axis=0)
    gathered = collect(coefficients, "win", 1)
    earlier = masked_gram(gathered, win_position * local_cols)
    window_ids = win_position * windows_here + jnp.arange(windows_here, dtype=jnp.int32)
    snap_totals = (snap_count * (window_ids + 1)).astype(jnp.float32)
    identity = jnp.eye(sketch_width, dtype=jnp.float32)
    prefix_grams = identity[None] + (earlier[None] + own_prefix) / snap_totals[:, None, None]
    return ortho_call(prefix_grams, coefficients.T, pivots)


def solution(mesh):
    placed = (P("dof", "win"), P("dof", None), P("win", None))
    return jax.shard_map(
        local,
        mesh=mesh,
        in_specs=placed,
        out_specs=(P("win", None), P("win", None, None)),
        check_vma=False,
    )
```

time: 96.7 us -> 56.4 us (0.58)
  other arithmetic: 43.8 us -> 0.83 us
  Pallas kernels: 0 us -> 6.67 us
  matrix products: 10.9 us -> 7.79 us
    another operation x12 -> x0, other arithmetic: 43.6 us -> none  [the longest x7 23.8 us: orthogonal(): chol_factor = jnp.linalg.cholesky(inner_gram)]
    pallas_call x0 -> x1, Pallas kernels: none -> 6.67 us  [ortho_call(): pl.pallas_call(ortho_kernel, out_shape=(jax.ShapeDtypeStruct((2, 64), jnp...]
    dot_general x6 -> x0, matrix products: 2.45 us -> none  [the longest x1 0.84 us: finish(): jnp.einsum('wkr,wks->wrs', basis_cols, window_blocks, precision=HIGHEST_P...]
  transfers between devices with their start and end apart: 1 -> 1, of which waited for: 1 -> 1; matrix products, arithmetic and copies ran while one was open for 0% -> 1% of each run, Pallas kernels for 0% -> 0%
where the time goes in v1:
time: 56.4 us; the launch traced here: 56.2 us
  blocking collectives  22.7 us (40%)
  waiting for transfers between devices  9.73 us (17%)
  matrix products  7.79 us (14%)
  starting transfers between devices  6.75 us (12%)
  Pallas kernels  6.67 us (12%)
  local copies, waits for them, and re-layouts  0.94 us (2%)
  other arithmetic  0.83 us (1%)
  between operations  0.7 us (1%)
    all_gather x1, blocking collectives, total_of_pieces(): return lax.all_gather(shard, axis).sum(0)  22.7 us
    all_to_all x1, waiting for transfers between devices, sent_to_all(): lax.all_to_all(jnp.broadcast_to(shard[None], (peers, *shard.shape)), axis...  9.73 us
    all_to_all x1, starting transfers between devices, sent_to_all(): lax.all_to_all(jnp.broadcast_to(shard[None], (peers, *shard.shape)), axis...  6.75 us
    pallas_call x1, Pallas kernels, ortho_call(): pl.pallas_call(ortho_kernel, out_shape=(jax.ShapeDtypeStruct((2, 64), jnp...  6.67 us
    dot_general x1, matrix products, local(): lax.dot_general(sketch_matrix, snapshots, (((0,), (0,)), ((), ())), prefe...  6.23 us
    dot_general x1, matrix products, masked_gram(): jnp.dot(gathered * keep_mask[None, :], gathered.T, precision=HIGHEST_PREC)  1.17 us
  transfers between devices with their start and end apart: 1, of which 1 were waited for; matrix products, arithmetic and copies ran while one was open for 1% of the time, Pallas kernels for 0%

profile of v1, /device:TPU:1, one launch (start us, length us, event | category | flops | bytes accessed | tf_op | source)
XLA Modules:
  0.0 56.2 jit_solution(7891315807860623714)
XLA Ops:
  0.6 6.2 %fusion.8 = f32[128,64]{0,1:T(8,128)S(1)} fusion(bf16[32768,64]{0,1:T(8,128)(2,1)} %param.3, bf16[32768,128]{1,0:T(8,128)(2,1)} %param.4), kind=kOutput, calls=%fused_computation.14 | convolution fusion | flops 536870912 | bytes 12615680 | tf_op jit(solution)/shard_map/dot_general | solution.py:174
  6.9 22.7 %all-gather = f32[2048,64]{0,1:T(8,128)S(1)} all-gather(f32[128,64]{0,1:T(8,128)S(1)} %fusion.8), channel_id=2, replica_groups=mesh['win'=16,'dof'=16] {'dof'}, dimensions={0}, use_global_device_ids=true | all-gather | bytes 557056 | tf_op jit(solution)/shard_map/all_gather | solution.py:141
  29.6 0.1 copy.5
  29.7 0.1 bitcast_reduce_fusion
  29.8 0.0 copy-start
  29.8 0.8 %broadcast_in_dim.2 = f32[16,128,64]{1,2,0:T(8,128)} broadcast(f32[128,64]{0,1:T(8,128)S(1)} %bitcast_reduce_fusion), dimensions={1,2} | broadcast | bytes 557056 | tf_op jit(solution)/shard_map/broadcast_in_dim | solution.py:147
  30.6 6.8 %all-to-all-start = ((f32[16,128,64]{1,2,0:T(8,128)}), f32[16,128,64]{1,2,0:T(8,128)S(1)}, u32[]{:S(2)}, u32[]{:S(2)}) async-start(f32[16,128,64]{1,2,0:T(8,128)} %broadcast_in_dim.2), calls=%async_computation | async-start | bytes 1048576 | tf_op jit(solution)/shard_map/all_to_all | solution.py:146
  37.5 0.4 fusion.7
  37.9 9.7 %all-to-all-done = f32[16,128,64]{1,2,0:T(8,128)S(1)} async-done(((f32[16,128,64]{1,2,0:T(8,128)}), f32[16,128,64]{1,2,0:T(8,128)S(1)}, u32[]{:S(2)}, u32[]{:S(2)}) %all-to-all-start) | async-done | bytes 524320 | tf_op jit(solution)/shard_map/all_to_all | solution.py:146
  47.6 1.2 %convolution_bitcast_fusion = f32[128,128]{1,0:T(8,128)S(1)} fusion(f32[16,128,64]{1,2,0:T(8,128)S(1)} %all-to-all-done, f32[16,64]{1,0:T(8,128)S(1)} %fusion.6), kind=kOutput, calls=%fused_computation.2 | convolution fusion | flops 201457664 | bytes 593920 | tf_op jit(solution)/shard_map/dot_general | solution.py:165
  48.8 0.7 %fusion.1.grams_ref = f32[2,128,128]{2,1,0:T(8,128)} fusion(f32[2,128,128]{2,1,0:T(8,128)S(1)} %fusion.7, f32[2]{0:T(128)S(1)} %multiply_convert_fusion, f32[128,128]{1,0:T(8,128)S(1)} %convolution_bitcast_fusion, f32[128,128]{1,0:T(8,128)S(1)} %fusion.5), kind=kOutput, calls=%fused_computation.3 | output fusion | flops 131072 | bytes 393224 | tf_op jit(solution)/shard_map/jit(cumsum)/reduce_window_sum | solution.py:182
  49.5 0.0 copy-done
  49.5 6.7 %shard_map.50 = (f32[2,64]{1,0:T(2,128)}, f32[2,32,64]{2,1,0:T(8,128)}) custom-call(f32[2,128,128]{2,1,0:T(8,128)} %fusion.1.grams_ref, f32[64,128]{1,0:T(8,128)} %bitcast.24, s32[2,64]{1,0:T(2,128)} %pivots_ref.1), custom_call_target="tpu_custom_call" | custom-call | tf_op jit(solution)/shard_map/pallas_call | solution.py:131
  (3 shorter events, 0.0 us)
Async XLA Ops:
  29.8 19.7 %copy-start = (f32[128,64]{0,1:T(8,128)}, f32[128,64]{0,1:T(8,128)S(1)}, u32[]{:S(2)}) copy-start(f32[128,64]{0,1:T(8,128)S(1)} %bitcast_reduce_fusion) | copy-start | bytes 98308
  30.6 16.9 %all-to-all-start = ((f32[16,128,64]{1,2,0:T(8,128)}), f32[16,128,64]{1,2,0:T(8,128)S(1)}, u32[]{:S(2)}, u32[]{:S(2)}) async-start(f32[16,128,64]{1,2,0:T(8,128)} %broadcast_in_dim.2), calls=%async_computation | async-start | bytes 1048576 | tf_op jit(solution)/shard_map/all_to_all | solution.py:146

commit v2 on v1

--- a/solution.py
+++ b/solution.py
@@ -118,75 +118,168 @@
     return jnp.sqrt(squares[:2]), proj
 
 
-def ortho_kernel(grams_ref, y_ref, pivots_ref, sing_ref, proj_ref):
+MESH = pl.DeviceIdType.MESH
+CHUNKS = 16
+
+
+def rdma(src, dst, send, recv, where):
+    return pltpu.make_async_remote_copy(
+        src_ref=src, dst_ref=dst, send_sem=send, recv_sem=recv, device_id=where, device_id_type=MESH
+    )
+
+
+def sum_kernel(stop, snap_hbm, sketch_hbm, own_ref, base_ref,
+               snap, sketch, part, rs_buf, ag_buf, gath, gram_send, gram_recv,
+               in_sem, rs_send, rs_recv, ag_send, ag_recv, xy_send, xy_recv, pair_sem):
+    d = lax.axis_index("dof")
+    w = lax.axis_index("win")
+    nd, nw = 16, 16
+    core = lax.rem(d, 2)
+    depth = sketch.shape[1]
+    loads = []
+    for i in range(CHUNKS):
+        a = pltpu.make_async_copy(sketch_hbm.at[pl.ds(i * depth, depth), :], sketch.at[i], in_sem.at[0, i])
+        b = pltpu.make_async_copy(snap_hbm.at[:, pl.ds(i * depth, depth)], snap.at[i], in_sem.at[1, i])
+        a.start()
+        b.start()
+        loads.append((a, b))
+    gath[...] = jnp.zeros_like(gath)
+    barrier = pltpu.get_barrier_semaphore()
+    for k in range(1, 16):
+        pl.semaphore_signal(barrier, inc=1, device_id={"dof": lax.rem(d + k, nd)}, device_id_type=MESH)
+        pl.semaphore_signal(barrier, inc=1, device_id={"win": lax.rem(w + k, nw)}, device_id_type=MESH)
+    total = jnp.zeros((64, 128), jnp.float32)
+    for i in range(CHUNKS):
+        for copy in loads[i]:
+            copy.wait()
+        total = total + jnp.dot(snap[i], sketch[i], preferred_element_type=jnp.float32)
+    for p in range(16):
+        part[p] = total[4 * p : 4 * p + 4, :]
+    pl.semaphore_wait(barrier, 30)
+    if stop < 1:
+        own_ref[...] = total
+        base_ref[...] = jnp.zeros_like(base_ref)
+        return
+    order = [8, 9, 7, 6, 10, 5, 11, 4, 12, 3, 13, 2, 14, 15, 1]
+    sends = []
+    for k in order:
+        q = lax.rem(d + k, nd)
+        copy = rdma(part.at[q], rs_buf.at[d], rs_send.at[k], rs_recv.at[d], {"dof": q})
+        copy.start()
+        sends.append(copy)
+    rs_buf[d] = part[d]
+    for k in reversed(order):
+        q = lax.rem(d + k, nd)
+        rdma(part.at[q], rs_buf.at[q], rs_send.at[k], rs_recv.at[q], {"dof": q}).wait_recv()
+    ag_buf[d] = jnp.sum(rs_buf[...], axis=0)
+    if stop >= 2:
+        for k in order:
+            q = lax.rem(d + k, nd)
+            copy = rdma(ag_buf.at[d], ag_buf.at[d], ag_send.at[k], ag_recv.at[d], {"dof": q})
+            copy.start()
+            sends.append(copy)
+    forwards = []
+
+    def forward(k, q):
+        z = q // 2
+        for v in range(16):
+            copy = rdma(ag_buf.at[q], gath.at[w, z], xy_send.at[k // 2, v], xy_recv.at[w, z], {"win": v})
+            forwards.append((v, copy))
+
+            @pl.when(v > w)
+            def _():
+                copy.start()
+
+    if stop >= 3:
+        forward(0, d)
+    if stop >= 2:
+        for k in reversed(order):
+            q = lax.rem(d + k, nd)
+            rdma(ag_buf.at[q], ag_buf.at[q], ag_send.at[k], ag_recv.at[q], {"dof": q}).wait_recv()
+            if stop >= 3 and k % 2 == 0:
+                forward(k, q)
+    if stop >= 3:
+        for v in range(16):
+            @pl.when(v < w)
+            def _():
+                for z in range(8):
+                    rdma(ag_buf.at[0], gath.at[v, z], xy_send.at[0, v], xy_recv.at[v, z], {"win": v}).wait_recv()
+    own_ref[...] = ag_buf[...].reshape(64, 128)
+    if stop >= 4:
+        x = gath[...].reshape(512, 128)
+        gram_send[...] = lax.dot_general(x, x, (((0,), (0,)), ((), ())), precision=lax.Precision.HIGHEST,
+                                         preferred_element_type=jnp.float32)
+        copy = rdma(gram_send, gram_recv, pair_sem.at[0], pair_sem.at[1], {"dof": d + 1 - 2 * core})
+        copy.start()
+        copy.wait()
+        base_ref[...] = gram_send[...] + gram_recv[...]
+    else:
+        base_ref[...] = jnp.sum(gath[...].reshape(4, 128, 128), axis=0)
+    for copy in sends:
+        copy.wait_send()
+    for v, copy in forwards:
+        @pl.when(v > w)
+        def _():
+            copy.wait_send()
+
+
+def sum_call(snapshots, sketch_matrix, stop=4):
+    depth = sketch_matrix.shape[0] // CHUNKS
+    f32 = jnp.float32
+    return pl.pallas_call(
+        functools.partial(sum_kernel, stop),
+        out_shape=(jax.ShapeDtypeStruct((64, 128), f32), jax.ShapeDtypeStruct((128, 128), f32)),
+        in_specs=[pl.BlockSpec(memory_space=pl.ANY)] * 2,
+        out_specs=(pl.BlockSpec(memory_space=pltpu.VMEM),) * 2,
+        scratch_shapes=[
+            pltpu.VMEM((CHUNKS, 64, depth), jnp.bfloat16),
+            pltpu.VMEM((CHUNKS, depth, 128), jnp.bfloat16),
+            pltpu.VMEM((16, 4, 128), f32),
+            pltpu.VMEM((16, 4, 128), f32),
+            pltpu.VMEM((16, 4, 128), f32),
+            pltpu.VMEM((16, 8, 4, 128), f32),
+            pltpu.VMEM((128, 128), f32),
+            pltpu.VMEM((128, 128), f32),
+            pltpu.SemaphoreType.DMA((2, CHUNKS)),
+            pltpu.SemaphoreType.DMA((16,)),
+            pltpu.SemaphoreType.DMA((16,)),
+            pltpu.SemaphoreType.DMA((16,)),
+            pltpu.SemaphoreType.DMA((16,)),
+            pltpu.SemaphoreType.DMA((8, 16)),
+            pltpu.SemaphoreType.DMA((16, 8)),
+            pltpu.SemaphoreType.DMA((2,)),
+        ],
+        compiler_params=pltpu.CompilerParams(collective_id=0, has_side_effects=True),
+    )(snapshots.T, sketch_matrix)
+
+def solve_kernel(own_ref, base_ref, pivots_ref, sing_ref, proj_ref):
+    w = lax.axis_index("win")
     piv = pivots_ref[...]
     piv_row = jnp.concatenate([piv[0:1, :], piv[1:2, :]], axis=1)
-    sing, proj = solve_windows(grams_ref[0], grams_ref[1], y_ref[:32, :], y_ref[32:, :], piv_row)
+    za, zb = own_ref[:32, :], own_ref[32:, :]
+    ma = lax.dot_general(za, za, (((0,), (0,)), ((), ())), precision=HIGHEST_PREC, preferred_element_type=jnp.float32)
+    mb = lax.dot_general(zb, zb, (((0,), (0,)), ((), ())), precision=HIGHEST_PREC, preferred_element_type=jnp.float32)
+    eye = jnp.where(
+        lax.broadcasted_iota(jnp.int32, (128, 128), 0) == lax.broadcasted_iota(jnp.int32, (128, 128), 1), 1.0, 0.0
+    )
+    count = jnp.full((128, 128), 64 * w, jnp.int32).astype(jnp.float32)
+    sa = base_ref[...] + ma
+    sb = sa + mb
+    sing, proj = solve_windows(eye + sa / (count + 32.0), eye + sb / (count + 64.0), za, zb, piv_row)
     sing_ref[...] = sing
     proj_ref[0] = proj[:, :64]
     proj_ref[1] = proj[:, 64:]
 
 
-def ortho_call(grams, yt, pivots):
+def local(snapshots, sketch_matrix, pivots):
+    own, base = sum_call(snapshots, sketch_matrix)
     sing, proj = pl.pallas_call(
-        ortho_kernel,
+        solve_kernel,
         out_shape=(jax.ShapeDtypeStruct((2, 64), jnp.float32), jax.ShapeDtypeStruct((2, 32, 64), jnp.float32)),
         in_specs=[pl.BlockSpec(memory_space=pltpu.VMEM)] * 3,
         out_specs=(pl.BlockSpec(memory_space=pltpu.VMEM),) * 2,
-    )(grams, yt, pivots)
+    )(own, base, pivots)
     return sing, jnp.swapaxes(proj, 1, 2)
-
-
-def total_of_pieces(shard, axis):
-    return lax.all_gather(shard, axis).sum(0)
-
-
-def sent_to_all(shard, axis):
-    peers = lax.axis_size(axis)
-    return lax.all_to_all(
-        jnp.broadcast_to(shard[None], (peers, *shard.shape)), axis, 0, 0, tiled=True
-    )
-
-
-def joined_along(parts, dim):
-    parts = jnp.moveaxis(parts, 0, dim)
-    lengths = parts.shape
-    return parts.reshape(*lengths[:dim], lengths[dim] * lengths[dim + 1], *lengths[dim + 2 :])
-
-
-def collect(shard, axis, dim):
-    parts = sent_to_all(shard, axis)
-    return joined_along(parts, dim)
-
-
-def masked_gram(gathered, limit):
-    column_ids = lax.iota(jnp.int32, gathered.shape[1])
-    keep_mask = (column_ids < limit).astype(jnp.float32)
-    return jnp.dot(gathered * keep_mask[None, :], gathered.T, precision=HIGHEST_PREC)
-
-
-def local(snapshots, sketch_matrix, pivots):
-    windows_here = pivots.shape[0]
-    sketch_width = sketch_matrix.shape[1]
-    local_cols = snapshots.shape[1]
-    snap_count = local_cols // windows_here
-    win_position = lax.axis_index("win")
-    partial_value = lax.dot_general(
-        sketch_matrix, snapshots, (((0,), (0,)), ((), ())), preferred_element_type=jnp.float32
-    )
-    coefficients = total_of_pieces(partial_value, "dof")
-    window_blocks = jnp.transpose(
-        coefficients.reshape(sketch_width, windows_here, snap_count), (1, 0, 2)
-    )
-    window_grams = jnp.einsum("wks,wjs->wkj", window_blocks, window_blocks, precision=HIGHEST_PREC)
-    own_prefix = jnp.cumsum(window_grams, axis=0)
-    gathered = collect(coefficients, "win", 1)
-    earlier = masked_gram(gathered, win_position * local_cols)
-    window_ids = win_position * windows_here + jnp.arange(windows_here, dtype=jnp.int32)
-    snap_totals = (snap_count * (window_ids + 1)).astype(jnp.float32)
-    identity = jnp.eye(sketch_width, dtype=jnp.float32)
-    prefix_grams = identity[None] + (earlier[None] + own_prefix) / snap_totals[:, None, None]
-    return ortho_call(prefix_grams, coefficients.T, pivots)
 
 
 def solution(mesh):

time: 56.4 us -> 36.7 us (0.65)
  the two profiles are of different devices: /device:TPU:1 before, /device:TPU:7 now
where the time goes in v2:
time: 36.7 us; the launch traced here: 36.5 us
  Pallas kernels  35.9 us (98%)
  between operations  0.64 us (2%)
    pallas_call x1, Pallas kernels, sum_call(): pl.pallas_call(functools.partial(sum_kernel, stop), out_shape=(jax.ShapeD...  29.1 us
    pallas_call x1, Pallas kernels, local(): pl.pallas_call(solve_kernel, out_shape=(jax.ShapeDtypeStruct((2, 64), jnp...  6.82 us

profile of v2, /device:TPU:7, one launch (start us, length us, event | category | flops | bytes accessed | tf_op | source)
XLA Modules:
  0.0 36.5 jit_solution(16315688227077205845)
XLA Ops:
  0.6 29.1 %shard_map.50 = (f32[64,128]{1,0:T(8,128)}, f32[128,128]{1,0:T(8,128)}) custom-call(bf16[64,32768]{1,0:T(8,128)(2,1)} %bitcast.2, bf16[32768,128]{1,0:T(8,128)(2,1)} %sketch_hbm.1), custom_call_target="tpu_custom_call" | custom-call | tf_op jit(solution)/shard_map/pallas_call | solution.py:229
  29.7 6.8 %shard_map.51 = (f32[2,64]{1,0:T(2,128)}, f32[2,32,64]{2,1,0:T(8,128)}) custom-call(f32[64,128]{1,0:T(8,128)} %get-tuple-element.6.own_ref, f32[128,128]{1,0:T(8,128)} %get-tuple-element.7.base_ref, s32[2,64]{1,0:T(2,128)} %pivots_ref.1), custom_call_target="tpu_custom_call" | custom-call | tf_op jit(solution)/shard_map/pallas_call | solution.py:276

commit v3 on v2

--- a/solution.py
+++ b/solution.py
@@ -119,7 +119,7 @@
 
 
 MESH = pl.DeviceIdType.MESH
-CHUNKS = 16
+CHUNKS = 8
 
 
 def rdma(src, dst, send, recv, where):
@@ -128,14 +128,27 @@
     )
 
 
-def sum_kernel(stop, snap_hbm, sketch_hbm, own_ref, base_ref,
-               snap, sketch, part, rs_buf, ag_buf, gath, gram_send, gram_recv,
-               in_sem, rs_send, rs_recv, ag_send, ag_recv, xy_send, xy_recv, pair_sem):
+def gram_of(x):
+    return lax.dot_general(
+        x, x, (((0,), (0,)), ((), ())), precision=lax.Precision.HIGHEST, preferred_element_type=jnp.float32
+    )
+
+
+def sum_kernel(snap_hbm, sketch_hbm, own_ref, grams_ref,
+               snap, sketch, part, rs_buf, ag_buf, gath, mate,
+               in_sem, rs_send, rs_recv, ag_send, ag_recv, xy_send, xy_recv, mate_send, mate_recv):
     d = lax.axis_index("dof")
     w = lax.axis_index("win")
     nd, nw = 16, 16
     core = lax.rem(d, 2)
+    partner = d + 1 - 2 * core
     depth = sketch.shape[1]
+    gath[...] = jnp.zeros_like(gath)
+    mate[...] = jnp.zeros_like(mate)
+    barrier = pltpu.get_barrier_semaphore()
+    for k in range(1, 16):
+        pl.semaphore_signal(barrier, inc=1, device_id={"dof": lax.rem(d + k, nd)}, device_id_type=MESH)
+        pl.semaphore_signal(barrier, inc=1, device_id={"win": lax.rem(w + k, nw)}, device_id_type=MESH)
     loads = []
     for i in range(CHUNKS):
         a = pltpu.make_async_copy(sketch_hbm.at[pl.ds(i * depth, depth), :], sketch.at[i], in_sem.at[0, i])
@@ -143,11 +156,6 @@
         a.start()
         b.start()
         loads.append((a, b))
-    gath[...] = jnp.zeros_like(gath)
-    barrier = pltpu.get_barrier_semaphore()
-    for k in range(1, 16):
-        pl.semaphore_signal(barrier, inc=1, device_id={"dof": lax.rem(d + k, nd)}, device_id_type=MESH)
-        pl.semaphore_signal(barrier, inc=1, device_id={"win": lax.rem(w + k, nw)}, device_id_type=MESH)
     total = jnp.zeros((64, 128), jnp.float32)
     for i in range(CHUNKS):
         for copy in loads[i]:
@@ -156,10 +164,6 @@
     for p in range(16):
         part[p] = total[4 * p : 4 * p + 4, :]
     pl.semaphore_wait(barrier, 30)
-    if stop < 1:
-        own_ref[...] = total
-        base_ref[...] = jnp.zeros_like(base_ref)
-        return
     order = [8, 9, 7, 6, 10, 5, 11, 4, 12, 3, 13, 2, 14, 15, 1]
     sends = []
     for k in order:
@@ -172,17 +176,16 @@
         q = lax.rem(d + k, nd)
         rdma(part.at[q], rs_buf.at[q], rs_send.at[k], rs_recv.at[q], {"dof": q}).wait_recv()
     ag_buf[d] = jnp.sum(rs_buf[...], axis=0)
-    if stop >= 2:
-        for k in order:
-            q = lax.rem(d + k, nd)
-            copy = rdma(ag_buf.at[d], ag_buf.at[d], ag_send.at[k], ag_recv.at[d], {"dof": q})
-            copy.start()
-            sends.append(copy)
+    for k in order:
+        q = lax.rem(d + k, nd)
+        copy = rdma(ag_buf.at[d], ag_buf.at[d], ag_send.at[k], ag_recv.at[d], {"dof": q})
+        copy.start()
+        sends.append(copy)
     forwards = []
 
     def forward(k, q):
         z = q // 2
-        for v in range(16):
+        for v in range(1, 16):
             copy = rdma(ag_buf.at[q], gath.at[w, z], xy_send.at[k // 2, v], xy_recv.at[w, z], {"win": v})
             forwards.append((v, copy))
 
@@ -190,31 +193,34 @@
             def _():
                 copy.start()
 
-    if stop >= 3:
-        forward(0, d)
-    if stop >= 2:
-        for k in reversed(order):
-            q = lax.rem(d + k, nd)
-            rdma(ag_buf.at[q], ag_buf.at[q], ag_send.at[k], ag_recv.at[q], {"dof": q}).wait_recv()
-            if stop >= 3 and k % 2 == 0:
-                forward(k, q)
-    if stop >= 3:
-        for v in range(16):
-            @pl.when(v < w)
-            def _():
-                for z in range(8):
-                    rdma(ag_buf.at[0], gath.at[v, z], xy_send.at[0, v], xy_recv.at[v, z], {"win": v}).wait_recv()
-    own_ref[...] = ag_buf[...].reshape(64, 128)
-    if stop >= 4:
-        x = gath[...].reshape(512, 128)
-        gram_send[...] = lax.dot_general(x, x, (((0,), (0,)), ((), ())), precision=lax.Precision.HIGHEST,
-                                         preferred_element_type=jnp.float32)
-        copy = rdma(gram_send, gram_recv, pair_sem.at[0], pair_sem.at[1], {"dof": d + 1 - 2 * core})
-        copy.start()
-        copy.wait()
-        base_ref[...] = gram_send[...] + gram_recv[...]
-    else:
-        base_ref[...] = jnp.sum(gath[...].reshape(4, 128, 128), axis=0)
+    forward(0, d)
+    for k in reversed(order):
+        q = lax.rem(d + k, nd)
+        rdma(ag_buf.at[q], ag_buf.at[q], ag_send.at[k], ag_recv.at[q], {"dof": q}).wait_recv()
+        if k % 2 == 0:
+            forward(k, q)
+    own = ag_buf[...].reshape(64, 128)
+    own_ref[...] = own
+    ma = gram_of(own[:32])
+    mab = ma + gram_of(own[32:])
+    for v in range(15):
+        @pl.when(v < w)
+        def _():
+            for z in range(8):
+                rdma(ag_buf.at[0], gath.at[v, z], xy_send.at[0, v], xy_recv.at[v, z], {"win": v}).wait_recv()
+            rdma(gath.at[v], mate.at[v], mate_send.at[v], mate_recv.at[v], {"dof": partner}).start()
+    base = gram_of(gath[...].reshape(512, 128))
+    for v in range(15):
+        @pl.when(v < w)
+        def _():
+            rdma(gath.at[v], mate.at[v], mate_send.at[v], mate_recv.at[v], {"dof": partner}).wait()
+    base = base + gram_of(mate[...].reshape(512, 128))
+    eye = jnp.where(
+        lax.broadcasted_iota(jnp.int32, (128, 128), 0) == lax.broadcasted_iota(jnp.int32, (128, 128), 1), 1.0, 0.0
+    )
+    count = jnp.full((128, 128), 64 * w, jnp.int32).astype(jnp.float32)
+    grams_ref[0] = eye + (base + ma) / (count + 32.0)
+    grams_ref[1] = eye + (base + mab) / (count + 64.0)
     for copy in sends:
         copy.wait_send()
     for v, copy in forwards:
@@ -227,9 +233,9 @@
     depth = sketch_matrix.shape[0] // CHUNKS
     f32 = jnp.float32
     return pl.pallas_call(
-        functools.partial(sum_kernel, stop),
-        out_shape=(jax.ShapeDtypeStruct((64, 128), f32), jax.ShapeDtypeStruct((128, 128), f32)),
-        in_specs=[pl.BlockSpec(memory_space=pl.ANY)] * 2,
+        sum_kernel,
+        out_shape=(jax.ShapeDtypeStruct((64, 128), f32), jax.ShapeDtypeStruct((2, 128, 128), f32)),
+        in_specs=[pl.BlockSpec(memory_space=pltpu.HBM)] * 2,
         out_specs=(pl.BlockSpec(memory_space=pltpu.VMEM),) * 2,
         scratch_shapes=[
             pltpu.VMEM((CHUNKS, 64, depth), jnp.bfloat16),
@@ -238,8 +244,7 @@
             pltpu.VMEM((16, 4, 128), f32),
             pltpu.VMEM((16, 4, 128), f32),
             pltpu.VMEM((16, 8, 4, 128), f32),
-            pltpu.VMEM((128, 128), f32),
-            pltpu.VMEM((128, 128), f32),
+            pltpu.VMEM((16, 8, 4, 128), f32),
             pltpu.SemaphoreType.DMA((2, CHUNKS)),
             pltpu.SemaphoreType.DMA((16,)),
             pltpu.SemaphoreType.DMA((16,)),
@@ -247,38 +252,30 @@
             pltpu.SemaphoreType.DMA((16,)),
             pltpu.SemaphoreType.DMA((8, 16)),
             pltpu.SemaphoreType.DMA((16, 8)),
-            pltpu.SemaphoreType.DMA((2,)),
+            pltpu.SemaphoreType.DMA((16,)),
+            pltpu.SemaphoreType.DMA((16,)),
         ],
-        compiler_params=pltpu.CompilerParams(collective_id=0, has_side_effects=True),
+        compiler_params=pltpu.CompilerParams(collective_id=0, has_side_effects=True, vmem_limit_bytes=52 * 1024 * 1024),
     )(snapshots.T, sketch_matrix)
 
-def solve_kernel(own_ref, base_ref, pivots_ref, sing_ref, proj_ref):
-    w = lax.axis_index("win")
+def solve_kernel(own_ref, grams_ref, pivots_ref, sing_ref, proj_ref):
     piv = pivots_ref[...]
     piv_row = jnp.concatenate([piv[0:1, :], piv[1:2, :]], axis=1)
-    za, zb = own_ref[:32, :], own_ref[32:, :]
-    ma = lax.dot_general(za, za, (((0,), (0,)), ((), ())), precision=HIGHEST_PREC, preferred_element_type=jnp.float32)
-    mb = lax.dot_general(zb, zb, (((0,), (0,)), ((), ())), precision=HIGHEST_PREC, preferred_element_type=jnp.float32)
-    eye = jnp.where(
-        lax.broadcasted_iota(jnp.int32, (128, 128), 0) == lax.broadcasted_iota(jnp.int32, (128, 128), 1), 1.0, 0.0
-    )
-    count = jnp.full((128, 128), 64 * w, jnp.int32).astype(jnp.float32)
-    sa = base_ref[...] + ma
-    sb = sa + mb
-    sing, proj = solve_windows(eye + sa / (count + 32.0), eye + sb / (count + 64.0), za, zb, piv_row)
+    sing, proj = solve_windows(grams_ref[0], grams_ref[1], own_ref[:32, :], own_ref[32:, :], piv_row)
     sing_ref[...] = sing
     proj_ref[0] = proj[:, :64]
     proj_ref[1] = proj[:, 64:]
 
 
 def local(snapshots, sketch_matrix, pivots):
-    own, base = sum_call(snapshots, sketch_matrix)
+    own, grams = sum_call(snapshots, sketch_matrix)
     sing, proj = pl.pallas_call(
         solve_kernel,
         out_shape=(jax.ShapeDtypeStruct((2, 64), jnp.float32), jax.ShapeDtypeStruct((2, 32, 64), jnp.float32)),
         in_specs=[pl.BlockSpec(memory_space=pltpu.VMEM)] * 3,
         out_specs=(pl.BlockSpec(memory_space=pltpu.VMEM),) * 2,
-    )(own, base, pivots)
+        compiler_params=pltpu.CompilerParams(vmem_limit_bytes=16 * 1024 * 1024),
+    )(own, grams, pivots)
     return sing, jnp.swapaxes(proj, 1, 2)
 
 

time: 36.7 us -> 35.7 us (0.973)
  Pallas kernels: 35.9 us -> 35 us
    pallas_call x1, Pallas kernels: 6.82 us -> 5.74 us  [local(): pl.pallas_call(solve_kernel, out_shape=(jax.ShapeDtypeStruct((2, 64), jnp...]
where the time goes in v3:
time: 35.7 us; the launch traced here: 35.6 us
  Pallas kernels  35 us (98%)
  between operations  0.65 us (2%)
    pallas_call x1, Pallas kernels, sum_call(): pl.pallas_call(sum_kernel, out_shape=(jax.ShapeDtypeStruct((64, 128), f32...  29.2 us
    pallas_call x1, Pallas kernels, local(): pl.pallas_call(solve_kernel, out_shape=(jax.ShapeDtypeStruct((2, 64), jnp...  5.74 us

profile of v3, /device:TPU:7, one launch (start us, length us, event | category | flops | bytes accessed | tf_op | source)
XLA Modules:
  0.0 35.6 jit_solution(13116700979384443897)
XLA Ops:
  0.6 0.0 copy-start
  0.6 29.2 %shard_map.50 = (f32[64,128]{1,0:T(8,128)S(1)}, f32[2,128,128]{2,1,0:T(8,128)S(1)}) custom-call(bf16[64,32768]{1,0:T(8,128)(2,1)} %bitcast.2, bf16[32768,128]{1,0:T(8,128)(2,1)} %sketch_hbm.1), custom_call_target="tpu_custom_call" | custom-call | tf_op jit(solution)/shard_map/pallas_call | solution.py:235
  29.9 0.0 copy-done
  29.9 5.7 %shard_map.51 = (f32[2,64]{1,0:T(2,128)}, f32[2,32,64]{2,1,0:T(8,128)}) custom-call(f32[64,128]{1,0:T(8,128)S(1)} %get-tuple-element.6.own_ref, f32[2,128,128]{2,1,0:T(8,128)S(1)} %get-tuple-element.7.grams_ref, s32[2,64]{1,0:T(2,128)S(1)} %copy-done), custom_call_target="tpu_custom_call" | custom-call | tf_op jit(solution)/shard_map/pallas_call | solution.py:272
Async XLA Ops:
  0.6 29.2 %copy-start = (s32[2,64]{1,0:T(2,128)S(1)}, s32[2,64]{1,0:T(2,128)}, u32[]{:S(2)}) copy-start(s32[2,64]{1,0:T(2,128)} %pivots_ref.1) | copy-start | bytes 1540

commit v4 on v3

--- a/solution.py
+++ b/solution.py
@@ -135,8 +135,8 @@
 
 
 def sum_kernel(snap_hbm, sketch_hbm, own_ref, grams_ref,
-               snap, sketch, part, rs_buf, ag_buf, gath, mate,
-               in_sem, rs_send, rs_recv, ag_send, ag_recv, xy_send, xy_recv, mate_send, mate_recv):
+               snap, sketch, part, rs_buf, ag_buf, gath, gram_send, gram_recv,
+               in_sem, rs_send, rs_recv, ag_send, ag_recv, ag_other, xy_send, xy_recv, pair_sem):
     d = lax.axis_index("dof")
     w = lax.axis_index("win")
     nd, nw = 16, 16
@@ -144,7 +144,6 @@
     partner = d + 1 - 2 * core
     depth = sketch.shape[1]
     gath[...] = jnp.zeros_like(gath)
-    mate[...] = jnp.zeros_like(mate)
     barrier = pltpu.get_barrier_semaphore()
     for k in range(1, 16):
         pl.semaphore_signal(barrier, inc=1, device_id={"dof": lax.rem(d + k, nd)}, device_id_type=MESH)
@@ -165,40 +164,34 @@
         part[p] = total[4 * p : 4 * p + 4, :]
     pl.semaphore_wait(barrier, 30)
     order = [8, 9, 7, 6, 10, 5, 11, 4, 12, 3, 13, 2, 14, 15, 1]
-    sends = []
     for k in order:
         q = lax.rem(d + k, nd)
-        copy = rdma(part.at[q], rs_buf.at[d], rs_send.at[k], rs_recv.at[d], {"dof": q})
-        copy.start()
-        sends.append(copy)
+        rdma(part.at[q], rs_buf.at[d], rs_send, rs_recv, {"dof": q}).start()
     rs_buf[d] = part[d]
-    for k in reversed(order):
-        q = lax.rem(d + k, nd)
-        rdma(part.at[q], rs_buf.at[q], rs_send.at[k], rs_recv.at[q], {"dof": q}).wait_recv()
+    fifteen = pl.ds(0, 15)
+    rdma(part.at[fifteen], rs_buf.at[fifteen], rs_send, rs_recv, {"dof": partner}).wait_recv()
     ag_buf[d] = jnp.sum(rs_buf[...], axis=0)
+    z_here = d // 2
     for k in order:
         q = lax.rem(d + k, nd)
-        copy = rdma(ag_buf.at[d], ag_buf.at[d], ag_send.at[k], ag_recv.at[d], {"dof": q})
-        copy.start()
-        sends.append(copy)
-    forwards = []
-
-    def forward(k, q):
+        arrival = ag_other if k % 2 else ag_recv.at[z_here]
+        rdma(ag_buf.at[d], ag_buf.at[d], ag_send, arrival, {"dof": q}).start()
+
+    def forward(q):
         z = q // 2
         for v in range(1, 16):
-            copy = rdma(ag_buf.at[q], gath.at[w, z], xy_send.at[k // 2, v], xy_recv.at[w, z], {"win": v})
-            forwards.append((v, copy))
-
             @pl.when(v > w)
             def _():
-                copy.start()
-
-    forward(0, d)
+                rdma(ag_buf.at[q], gath.at[w, z], xy_send.at[v], xy_recv.at[w], {"win": v}).start()
+
+    forward(d)
     for k in reversed(order):
-        q = lax.rem(d + k, nd)
-        rdma(ag_buf.at[q], ag_buf.at[q], ag_send.at[k], ag_recv.at[q], {"dof": q}).wait_recv()
         if k % 2 == 0:
-            forward(k, q)
+            q = lax.rem(d + k, nd)
+            rdma(ag_buf.at[q], ag_buf.at[q], ag_send, ag_recv.at[q // 2], {"dof": q}).wait_recv()
+            forward(q)
+    eight = pl.ds(0, 8)
+    rdma(ag_buf.at[eight], ag_buf.at[eight], ag_send, ag_other, {"dof": partner}).wait_recv()
     own = ag_buf[...].reshape(64, 128)
     own_ref[...] = own
     ma = gram_of(own[:32])
@@ -206,27 +199,24 @@
     for v in range(15):
         @pl.when(v < w)
         def _():
-            for z in range(8):
-                rdma(ag_buf.at[0], gath.at[v, z], xy_send.at[0, v], xy_recv.at[v, z], {"win": v}).wait_recv()
-            rdma(gath.at[v], mate.at[v], mate_send.at[v], mate_recv.at[v], {"dof": partner}).start()
-    base = gram_of(gath[...].reshape(512, 128))
-    for v in range(15):
-        @pl.when(v < w)
+            rdma(gath.at[v], gath.at[v], xy_send.at[v], xy_recv.at[v], {"win": v}).wait_recv()
+    gram_send[...] = gram_of(gath[...].reshape(512, 128))
+    swap = rdma(gram_send, gram_recv, pair_sem.at[0], pair_sem.at[1], {"dof": partner})
+    swap.start()
+    rdma(part.at[fifteen], rs_buf.at[fifteen], rs_send, rs_recv, {"dof": partner}).wait_send()
+    rdma(ag_buf.at[fifteen], ag_buf.at[fifteen], ag_send, ag_other, {"dof": partner}).wait_send()
+    for v in range(1, 16):
+        @pl.when(v > w)
         def _():
-            rdma(gath.at[v], mate.at[v], mate_send.at[v], mate_recv.at[v], {"dof": partner}).wait()
-    base = base + gram_of(mate[...].reshape(512, 128))
+            rdma(ag_buf.at[eight], gath.at[w], xy_send.at[v], xy_recv.at[v], {"win": v}).wait_send()
     eye = jnp.where(
         lax.broadcasted_iota(jnp.int32, (128, 128), 0) == lax.broadcasted_iota(jnp.int32, (128, 128), 1), 1.0, 0.0
     )
     count = jnp.full((128, 128), 64 * w, jnp.int32).astype(jnp.float32)
+    swap.wait()
+    base = gram_send[...] + gram_recv[...]
     grams_ref[0] = eye + (base + ma) / (count + 32.0)
     grams_ref[1] = eye + (base + mab) / (count + 64.0)
-    for copy in sends:
-        copy.wait_send()
-    for v, copy in forwards:
-        @pl.when(v > w)
-        def _():
-            copy.wait_send()
 
 
 def sum_call(snapshots, sketch_matrix, stop=4):
@@ -235,7 +225,7 @@
     return pl.pallas_call(
         sum_kernel,
         out_shape=(jax.ShapeDtypeStruct((64, 128), f32), jax.ShapeDtypeStruct((2, 128, 128), f32)),
-        in_specs=[pl.BlockSpec(memory_space=pltpu.HBM)] * 2,
+        in_specs=[pl.BlockSpec(memory_space=pl.ANY)] * 2,
         out_specs=(pl.BlockSpec(memory_space=pltpu.VMEM),) * 2,
         scratch_shapes=[
             pltpu.VMEM((CHUNKS, 64, depth), jnp.bfloat16),
@@ -244,16 +234,17 @@
             pltpu.VMEM((16, 4, 128), f32),
             pltpu.VMEM((16, 4, 128), f32),
             pltpu.VMEM((16, 8, 4, 128), f32),
-            pltpu.VMEM((16, 8, 4, 128), f32),
+            pltpu.VMEM((128, 128), f32),
+            pltpu.VMEM((128, 128), f32),
             pltpu.SemaphoreType.DMA((2, CHUNKS)),
+            pltpu.SemaphoreType.DMA,
+            pltpu.SemaphoreType.DMA,
+            pltpu.SemaphoreType.DMA,
+            pltpu.SemaphoreType.DMA((8,)),
+            pltpu.SemaphoreType.DMA,
             pltpu.SemaphoreType.DMA((16,)),
-            pltpu.SemaphoreType.DMA((16,)),
-            pltpu.SemaphoreType.DMA((16,)),
-            pltpu.SemaphoreType.DMA((16,)),
-            pltpu.SemaphoreType.DMA((8, 16)),
-            pltpu.SemaphoreType.DMA((16, 8)),
-            pltpu.SemaphoreType.DMA((16,)),
-            pltpu.SemaphoreType.DMA((16,)),
+            pltpu.SemaphoreType.DMA((15,)),
+            pltpu.SemaphoreType.DMA((2,)),
         ],
         compiler_params=pltpu.CompilerParams(collective_id=0, has_side_effects=True, vmem_limit_bytes=52 * 1024 * 1024),
     )(snapshots.T, sketch_matrix)

time: 35.7 us -> 32.2 us (0.902)
  Pallas kernels: 35 us -> 31.4 us
    pallas_call x1, Pallas kernels: 29.2 us -> 25.7 us  [sum_call(): pl.pallas_call(sum_kernel, out_shape=(jax.ShapeDtypeStruct((64, 128), f32...]
where the time goes in v4:
time: 32.2 us; the launch traced here: 32.1 us
  Pallas kernels  31.4 us (98%)
  between operations  0.65 us (2%)
    pallas_call x1, Pallas kernels, sum_call(): pl.pallas_call(sum_kernel, out_shape=(jax.ShapeDtypeStruct((64, 128), f32...  25.7 us
    pallas_call x1, Pallas kernels, local(): pl.pallas_call(solve_kernel, out_shape=(jax.ShapeDtypeStruct((2, 64), jnp...  5.74 us

profile of v4, /device:TPU:7, one launch (start us, length us, event | category | flops | bytes accessed | tf_op | source)
XLA Modules:
  0.0 32.1 jit_solution(14851583119622712988)
XLA Ops:
  0.6 0.0 copy-start
  0.6 25.7 %shard_map.50 = (f32[64,128]{1,0:T(8,128)S(1)}, f32[2,128,128]{2,1,0:T(8,128)S(1)}) custom-call(bf16[64,32768]{1,0:T(8,128)(2,1)} %bitcast.2, bf16[32768,128]{1,0:T(8,128)(2,1)} %sketch_hbm.1), custom_call_target="tpu_custom_call" | custom-call | tf_op jit(solution)/shard_map/pallas_call | solution.py:225
  26.4 0.0 copy-done
  26.4 5.7 %shard_map.51 = (f32[2,64]{1,0:T(2,128)}, f32[2,32,64]{2,1,0:T(8,128)}) custom-call(f32[64,128]{1,0:T(8,128)S(1)} %get-tuple-element.6.own_ref, f32[2,128,128]{2,1,0:T(8,128)S(1)} %get-tuple-element.7.grams_ref, s32[2,64]{1,0:T(2,128)S(1)} %copy-done), custom_call_target="tpu_custom_call" | custom-call | tf_op jit(solution)/shard_map/pallas_call | solution.py:263
Async XLA Ops:
  0.6 25.7 %copy-start = (s32[2,64]{1,0:T(2,128)S(1)}, s32[2,64]{1,0:T(2,128)}, u32[]{:S(2)}) copy-start(s32[2,64]{1,0:T(2,128)} %pivots_ref.1) | copy-start | bytes 1540

commit v5 on v4

--- a/solution.py
+++ b/solution.py
@@ -33,31 +33,45 @@
     lane = lax.broadcasted_iota(jnp.int32, (8, 128), 1)
     sub = lax.broadcasted_iota(jnp.int32, (8, 128), 0)
     base = lane - lane % 64
-    v0, v1, v2 = split_rows(gram), split_rows(low), split_rows(high)
+    v0, v1, v2 = split_rows(gram * 2.0**-32), split_rows(low), split_rows(high)
+
+    def bcast(x, p):
+        return jnp.broadcast_to(x[p : p + 1, :], (8, 128))
+
     for kb in range(8):
         cols = []
         for j in range(8):
             idx = base + (8 * kb + j)
             cols.append({i: jnp.take_along_axis(v0[i], idx, axis=1) for i in range(kb, 8)})
-        diag = cols[0][kb]
-        for p in range(8):
-            pivot = jnp.broadcast_to(cols[p][kb][p : p + 1, :], (8, 128))
-            if p:
-                diag = jnp.where(sub >= p, pivot, diag)
-            else:
-                diag = pivot
-            inv = 1.0 / pivot
-            mult = {i: cols[p][i] * inv for i in range(kb, 8)}
-            mult[kb] = jnp.where(sub > p, mult[kb], 0.0)
-            for j in range(p + 1, 8):
-                row = jnp.broadcast_to(cols[j][kb][p : p + 1, :], (8, 128))
+        diag = None
+        for p in range(0, 8, 2):
+            q = p + 1
+            cp, cq = cols[p], cols[q]
+            a, b, c = bcast(cp[kb], p), bcast(cp[kb], q), bcast(cq[kb], q)
+            det = a * c - b * b
+            inv = 1.0 / det
+            inv_a = 1.0 / a
+            m1, m2 = {}, {}
+            for i in range(kb, 8):
+                n1 = cp[i] * c - cq[i] * b
+                n2 = cq[i] * a - cp[i] * b
+                if i == kb:
+                    n1 = jnp.where(sub > q, n1, 0.0)
+                    n2 = jnp.where(sub > q, n2, 0.0)
+                m1[i], m2[i] = n1 * inv, n2 * inv
+            m1[kb] = jnp.where(sub == q, b * inv_a, m1[kb])
+            dq = det * inv_a
+            diag = a if diag is None else jnp.where(sub >= p, a, diag)
+            diag = jnp.where(sub >= q, dq, diag)
+            for j in range(q + 1, 8):
+                rp, rq = bcast(cols[j][kb], p), bcast(cols[j][kb], q)
                 for i in range(kb, 8):
-                    cols[j][i] = cols[j][i] - mult[i] * row
+                    cols[j][i] = cols[j][i] - (m1[i] * rp + m2[i] * rq)
             for v in (v0, v1, v2) if kb < 7 else (v1, v2):
-                row = jnp.broadcast_to(v[kb][p : p + 1, :], (8, 128))
+                rp, rq = bcast(v[kb], p), bcast(v[kb], q)
                 for i in range(kb, 8):
-                    v[i] = v[i] - mult[i] * row
-        scale = lax.rsqrt(diag)
+                    v[i] = v[i] - (m1[i] * rp + m2[i] * rq)
+        scale = lax.rsqrt(diag) * 2.0**-16
         v1[kb] = v1[kb] * scale
         v2[kb] = v2[kb] * scale
     return jnp.concatenate(v1, axis=0), jnp.concatenate(v2, axis=0)
@@ -132,6 +146,18 @@
     return lax.dot_general(
         x, x, (((0,), (0,)), ((), ())), precision=lax.Precision.HIGHEST, preferred_element_type=jnp.float32
     )
+
+
+def gram_split(x):
+    high = x.astype(jnp.bfloat16)
+    low = (x - high.astype(jnp.float32)).astype(jnp.bfloat16)
+    both = jnp.concatenate([high, low], axis=1)
+    g = lax.dot_general(both, both, (((0,), (0,)), ((), ())), preferred_element_type=jnp.float32)
+    return (g[:128, :128] + g[128:, 128:]) + (g[:128, 128:] + g[128:, :128])
+
+
+def slot_of(q):
+    return lax.rem(q, 2) * 8 + q // 2
 
 
 def sum_kernel(snap_hbm, sketch_hbm, own_ref, grams_ref,
@@ -163,33 +189,40 @@
     for p in range(16):
         part[p] = total[4 * p : 4 * p + 4, :]
     pl.semaphore_wait(barrier, 30)
+    me = slot_of(d)
     order = [8, 9, 7, 6, 10, 5, 11, 4, 12, 3, 13, 2, 14, 15, 1]
     for k in order:
         q = lax.rem(d + k, nd)
-        rdma(part.at[q], rs_buf.at[d], rs_send, rs_recv, {"dof": q}).start()
-    rs_buf[d] = part[d]
+        rdma(part.at[slot_of(q)], rs_buf.at[me], rs_send, rs_recv, {"dof": q}).start()
+    rs_buf[me] = part[me]
     fifteen = pl.ds(0, 15)
     rdma(part.at[fifteen], rs_buf.at[fifteen], rs_send, rs_recv, {"dof": partner}).wait_recv()
-    ag_buf[d] = jnp.sum(rs_buf[...], axis=0)
+    ag_buf[me] = jnp.sum(rs_buf[...], axis=0)
     z_here = d // 2
     for k in order:
         q = lax.rem(d + k, nd)
         arrival = ag_other if k % 2 else ag_recv.at[z_here]
-        rdma(ag_buf.at[d], ag_buf.at[d], ag_send, arrival, {"dof": q}).start()
-
-    def forward(q):
-        z = q // 2
-        for v in range(1, 16):
-            @pl.when(v > w)
-            def _():
-                rdma(ag_buf.at[q], gath.at[w, z], xy_send.at[v], xy_recv.at[w], {"win": v}).start()
-
-    forward(d)
+        rdma(ag_buf.at[me], ag_buf.at[me], ag_send, arrival, {"dof": q}).start()
+
+    def wait_piece(q):
+        rdma(ag_buf.at[slot_of(q)], ag_buf.at[slot_of(q)], ag_send, ag_recv.at[q // 2], {"dof": q}).wait_recv()
+
+    def forward(first, count):
+        src = ag_buf.at[pl.ds(core * 8 + first, count)]
+        dst = gath.at[w, pl.ds(first, count)]
+
+        def send(v, carry):
+            rdma(src, dst, xy_send.at[v], xy_recv.at[w], {"win": v}).start()
+            return carry
+
+        lax.fori_loop(w + 1, 16, send, 0)
+
+    forward(z_here, 1)
     for k in reversed(order):
         if k % 2 == 0:
             q = lax.rem(d + k, nd)
-            rdma(ag_buf.at[q], ag_buf.at[q], ag_send, ag_recv.at[q // 2], {"dof": q}).wait_recv()
-            forward(q)
+            wait_piece(q)
+            forward(q // 2, 1)
     eight = pl.ds(0, 8)
     rdma(ag_buf.at[eight], ag_buf.at[eight], ag_send, ag_other, {"dof": partner}).wait_recv()
     own = ag_buf[...].reshape(64, 128)
@@ -200,7 +233,7 @@
         @pl.when(v < w)
         def _():
             rdma(gath.at[v], gath.at[v], xy_send.at[v], xy_recv.at[v], {"win": v}).wait_recv()
-    gram_send[...] = gram_of(gath[...].reshape(512, 128))
+    gram_send[...] = gram_split(gath[...].reshape(512, 128))
     swap = rdma(gram_send, gram_recv, pair_sem.at[0], pair_sem.at[1], {"dof": partner})
     swap.start()
     rdma(part.at[fifteen], rs_buf.at[fifteen], rs_send, rs_recv, {"dof": partner}).wait_send()
@@ -219,7 +252,7 @@
     grams_ref[1] = eye + (base + mab) / (count + 64.0)
 
 
-def sum_call(snapshots, sketch_matrix, stop=4):
+def sum_call(snapshots, sketch_matrix):
     depth = sketch_matrix.shape[0] // CHUNKS
     f32 = jnp.float32
     return pl.pallas_call(
@@ -243,7 +276,7 @@
             pltpu.SemaphoreType.DMA((8,)),
             pltpu.SemaphoreType.DMA,
             pltpu.SemaphoreType.DMA((16,)),
-            pltpu.SemaphoreType.DMA((15,)),
+            pltpu.SemaphoreType.DMA((16,)),
             pltpu.SemaphoreType.DMA((2,)),
         ],
         compiler_params=pltpu.CompilerParams(collective_id=0, has_side_effects=True, vmem_limit_bytes=52 * 1024 * 1024),

time: 32.2 us -> 31.1 us (0.966)
  Pallas kernels: 31.4 us -> 30.4 us
    pallas_call x1, Pallas kernels: 5.74 us -> 4.78 us  [local(): pl.pallas_call(solve_kernel, out_shape=(jax.ShapeDtypeStruct((2, 64), jnp...]
where the time goes in v5:
time: 31.1 us; the launch traced here: 31 us
  Pallas kernels  30.4 us (98%)
  between operations  0.65 us (2%)
    pallas_call x1, Pallas kernels, sum_call(): pl.pallas_call(sum_kernel, out_shape=(jax.ShapeDtypeStruct((64, 128), f32...  25.6 us
    pallas_call x1, Pallas kernels, local(): pl.pallas_call(solve_kernel, out_shape=(jax.ShapeDtypeStruct((2, 64), jnp...  4.78 us

profile of v5, /device:TPU:7, one launch (start us, length us, event | category | flops | bytes accessed | tf_op | source)
XLA Modules:
  0.0 31.0 jit_solution(2060715934068544121)
XLA Ops:
  0.6 0.0 copy-start
  0.6 25.6 %shard_map.50 = (f32[64,128]{1,0:T(8,128)S(1)}, f32[2,128,128]{2,1,0:T(8,128)S(1)}) custom-call(bf16[64,32768]{1,0:T(8,128)(2,1)} %bitcast.2, bf16[32768,128]{1,0:T(8,128)(2,1)} %sketch_hbm.1), custom_call_target="tpu_custom_call" | custom-call | tf_op jit(solution)/shard_map/pallas_call | solution.py:258
  26.2 0.0 copy-done
  26.3 4.8 %shard_map.51 = (f32[2,64]{1,0:T(2,128)}, f32[2,32,64]{2,1,0:T(8,128)}) custom-call(f32[64,128]{1,0:T(8,128)S(1)} %get-tuple-element.6.own_ref, f32[2,128,128]{2,1,0:T(8,128)S(1)} %get-tuple-element.7.grams_ref, s32[2,64]{1,0:T(2,128)S(1)} %copy-done), custom_call_target="tpu_custom_call" | custom-call | tf_op jit(solution)/shard_map/pallas_call | solution.py:296
Async XLA Ops:
  0.6 25.6 %copy-start = (s32[2,64]{1,0:T(2,128)S(1)}, s32[2,64]{1,0:T(2,128)}, u32[]{:S(2)}) copy-start(s32[2,64]{1,0:T(2,128)} %pivots_ref.1) | copy-start | bytes 1540

commit v6 on v5

--- a/solution.py
+++ b/solution.py
@@ -29,11 +29,17 @@
     return [x[8 * i : 8 * i + 8, :] for i in range(8)]
 
 
-def whiten(gram, low, high):
+def whiten(gram, *payload):
     lane = lax.broadcasted_iota(jnp.int32, (8, 128), 1)
     sub = lax.broadcasted_iota(jnp.int32, (8, 128), 0)
     base = lane - lane % 64
-    v0, v1, v2 = split_rows(gram * 2.0**-32), split_rows(low), split_rows(high)
+    small = 2.0**-32
+    if gram is None:
+        rows = [split_rows(x * small) for x in payload]
+        pivots_from, unit = rows[0], 2.0**16
+    else:
+        rows = [split_rows(x) for x in payload]
+        pivots_from, unit = split_rows(gram * small), 2.0**-16
 
     def bcast(x, p):
         return jnp.broadcast_to(x[p : p + 1, :], (8, 128))
@@ -42,7 +48,7 @@
         cols = []
         for j in range(8):
             idx = base + (8 * kb + j)
-            cols.append({i: jnp.take_along_axis(v0[i], idx, axis=1) for i in range(kb, 8)})
+            cols.append({i: jnp.take_along_axis(pivots_from[i], idx, axis=1) for i in range(kb, 8)})
         diag = None
         for p in range(0, 8, 2):
             q = p + 1
@@ -67,14 +73,14 @@
                 rp, rq = bcast(cols[j][kb], p), bcast(cols[j][kb], q)
                 for i in range(kb, 8):
                     cols[j][i] = cols[j][i] - (m1[i] * rp + m2[i] * rq)
-            for v in (v0, v1, v2) if kb < 7 else (v1, v2):
+            for v in rows if gram is None or kb == 7 else [pivots_from] + rows:
                 rp, rq = bcast(v[kb], p), bcast(v[kb], q)
                 for i in range(kb, 8):
                     v[i] = v[i] - (m1[i] * rp + m2[i] * rq)
-        scale = lax.rsqrt(diag) * 2.0**-16
-        v1[kb] = v1[kb] * scale
-        v2[kb] = v2[kb] * scale
-    return jnp.concatenate(v1, axis=0), jnp.concatenate(v2, axis=0)
+        scale = lax.rsqrt(diag) * unit
+        for v in rows:
+            v[kb] = v[kb] * scale
+    return [jnp.concatenate(v, axis=0) for v in rows]
 
 
 def masked_pair(low, high):
@@ -104,13 +110,10 @@
         ],
         axis=0,
     )
-    low, high = lo_a, hi_a
-    for sweep in range(2):
-        if sweep:
-            image = dot_nn(jnp.concatenate([low, high], axis=1), joint)
-            low, high = image[:, :128], image[:, 128:]
-        gram = dot_nt(jnp.concatenate([low, high], axis=1), masked_pair(low, high))
-        low, high = whiten(gram, low, high)
+    square = dot_nn(jnp.concatenate([lo_a, hi_a], axis=1), joint)
+    low, high = whiten(None, square[:, :128], square[:, 128:])
+    gram = dot_nt(jnp.concatenate([low, high], axis=1), masked_pair(low, high))
+    low, high = whiten(gram, low, high)
     basis = jnp.concatenate([low, high], axis=1)
     image = dot_nn(basis, joint)
     prod = basis * image
@@ -169,11 +172,6 @@
     core = lax.rem(d, 2)
     partner = d + 1 - 2 * core
     depth = sketch.shape[1]
-    gath[...] = jnp.zeros_like(gath)
-    barrier = pltpu.get_barrier_semaphore()
-    for k in range(1, 16):
-        pl.semaphore_signal(barrier, inc=1, device_id={"dof": lax.rem(d + k, nd)}, device_id_type=MESH)
-        pl.semaphore_signal(barrier, inc=1, device_id={"win": lax.rem(w + k, nw)}, device_id_type=MESH)
     loads = []
     for i in range(CHUNKS):
         a = pltpu.make_async_copy(sketch_hbm.at[pl.ds(i * depth, depth), :], sketch.at[i], in_sem.at[0, i])
@@ -181,6 +179,11 @@
         a.start()
         b.start()
         loads.append((a, b))
+    gath[...] = jnp.zeros_like(gath)
+    barrier = pltpu.get_barrier_semaphore()
+    for k in range(1, 16):
+        pl.semaphore_signal(barrier, inc=1, device_id={"dof": lax.rem(d + k, nd)}, device_id_type=MESH)
+        pl.semaphore_signal(barrier, inc=1, device_id={"win": lax.rem(w + k, nw)}, device_id_type=MESH)
     total = jnp.zeros((64, 128), jnp.float32)
     for i in range(CHUNKS):
         for copy in loads[i]:
@@ -229,6 +232,12 @@
     own_ref[...] = own
     ma = gram_of(own[:32])
     mab = ma + gram_of(own[32:])
+    eye = jnp.where(
+        lax.broadcasted_iota(jnp.int32, (128, 128), 0) == lax.broadcasted_iota(jnp.int32, (128, 128), 1), 1.0, 0.0
+    )
+    count = jnp.full((128, 128), 64 * w, jnp.int32).astype(jnp.float32)
+    inv_a, inv_b = 1.0 / (count + 32.0), 1.0 / (count + 64.0)
+    own_a, own_b = eye + ma * inv_a, eye + mab * inv_b
     for v in range(15):
         @pl.when(v < w)
         def _():
@@ -242,14 +251,10 @@
         @pl.when(v > w)
         def _():
             rdma(ag_buf.at[eight], gath.at[w], xy_send.at[v], xy_recv.at[v], {"win": v}).wait_send()
-    eye = jnp.where(
-        lax.broadcasted_iota(jnp.int32, (128, 128), 0) == lax.broadcasted_iota(jnp.int32, (128, 128), 1), 1.0, 0.0
-    )
-    count = jnp.full((128, 128), 64 * w, jnp.int32).astype(jnp.float32)
     swap.wait()
     base = gram_send[...] + gram_recv[...]
-    grams_ref[0] = eye + (base + ma) / (count + 32.0)
-    grams_ref[1] = eye + (base + mab) / (count + 64.0)
+    grams_ref[0] = own_a + base * inv_a
+    grams_ref[1] = own_b + base * inv_b
 
 
 def sum_call(snapshots, sketch_matrix):

time: 31.1 us -> 30.4 us (0.977)
  Pallas kernels: 30.4 us -> 29.7 us
    pallas_call x1, Pallas kernels: 25.6 us -> 25.2 us  [sum_call(): pl.pallas_call(sum_kernel, out_shape=(jax.ShapeDtypeStruct((64, 128), f32...]
where the time goes in v6:
time: 30.4 us; the launch traced here: 30.3 us
  Pallas kernels  29.7 us (98%)
  between operations  0.65 us (2%)
    pallas_call x1, Pallas kernels, sum_call(): pl.pallas_call(sum_kernel, out_shape=(jax.ShapeDtypeStruct((64, 128), f32...  25.2 us
    pallas_call x1, Pallas kernels, local(): pl.pallas_call(solve_kernel, out_shape=(jax.ShapeDtypeStruct((2, 64), jnp...  4.48 us

profile of v6, /device:TPU:7, one launch (start us, length us, event | category | flops | bytes accessed | tf_op | source)
XLA Modules:
  0.0 30.3 jit_solution(10784746193664569075)
XLA Ops:
  0.6 0.0 copy-start
  0.6 25.2 %shard_map.50 = (f32[64,128]{1,0:T(8,128)S(1)}, f32[2,128,128]{2,1,0:T(8,128)S(1)}) custom-call(bf16[64,32768]{1,0:T(8,128)(2,1)} %bitcast.2, bf16[32768,128]{1,0:T(8,128)(2,1)} %sketch_hbm.1), custom_call_target="tpu_custom_call" | custom-call | tf_op jit(solution)/shard_map/pallas_call | solution.py:263
  25.8 0.0 copy-done
  25.8 4.5 %shard_map.51 = (f32[2,64]{1,0:T(2,128)}, f32[2,32,64]{2,1,0:T(8,128)}) custom-call(f32[64,128]{1,0:T(8,128)S(1)} %get-tuple-element.6.own_ref, f32[2,128,128]{2,1,0:T(8,128)S(1)} %get-tuple-element.7.grams_ref, s32[2,64]{1,0:T(2,128)S(1)} %copy-done), custom_call_target="tpu_custom_call" | custom-call | tf_op jit(solution)/shard_map/pallas_call | solution.py:301
Async XLA Ops:
  0.6 25.2 %copy-start = (s32[2,64]{1,0:T(2,128)S(1)}, s32[2,64]{1,0:T(2,128)}, u32[]{:S(2)}) copy-start(s32[2,64]{1,0:T(2,128)} %pivots_ref.1) | copy-start | bytes 1540

commit v7 on v6

--- a/solution.py
+++ b/solution.py
@@ -19,6 +19,30 @@
 
 def dot_nn(a, b):
     return lax.dot_general(a, b, (((1,), (0,)), ((), ())), precision=HIGHEST_PREC, preferred_element_type=jnp.float32)
+
+
+def dot_bf16(a, b, dims=(((1,), (0,)), ((), ()))):
+    return lax.dot_general(a, b, dims, preferred_element_type=jnp.float32)
+
+
+def two_terms(x):
+    high = x.astype(jnp.bfloat16)
+    return high, (x - high.astype(jnp.float32)).astype(jnp.bfloat16)
+
+
+def three_terms(x):
+    high = x.astype(jnp.bfloat16)
+    rest = x - high.astype(jnp.float32)
+    mid = rest.astype(jnp.bfloat16)
+    return high, mid, (rest - mid.astype(jnp.float32)).astype(jnp.bfloat16)
+
+
+def dot_full(a, b, dims=(((1,), (0,)), ((), ()))):
+    rows = a[0].shape[0]
+    x = dot_bf16(jnp.concatenate(a, axis=0), b[0], dims)
+    y = dot_bf16(jnp.concatenate(a[:2], axis=0), b[1], dims)
+    z = dot_bf16(a[0], b[2], dims)
+    return x[:rows] + ((x[rows : 2 * rows] + y[:rows]) + (x[2 * rows :] + y[rows:] + z))
 
 
 def halves(a, b):
@@ -85,7 +109,7 @@
 
 def masked_pair(low, high):
     first = lax.broadcasted_iota(jnp.int32, (64, 128), 1) < 64
-    zero = jnp.zeros((64, 128), jnp.float32)
+    zero = jnp.zeros((64, 128), low.dtype)
     top = jnp.concatenate([jnp.where(first, low, zero), jnp.where(first, high, zero)], axis=1)
     bottom = jnp.concatenate([jnp.where(first, zero, low), jnp.where(first, zero, high)], axis=1)
     return jnp.concatenate([top, bottom], axis=0)
@@ -110,28 +134,39 @@
         ],
         axis=0,
     )
-    square = dot_nn(jnp.concatenate([lo_a, hi_a], axis=1), joint)
-    low, high = whiten(None, square[:, :128], square[:, 128:])
-    gram = dot_nt(jnp.concatenate([low, high], axis=1), masked_pair(low, high))
-    low, high = whiten(gram, low, high)
-    basis = jnp.concatenate([low, high], axis=1)
-    image = dot_nn(basis, joint)
-    prod = basis * image
-    first = lax.broadcasted_iota(jnp.int32, (8, 256), 1) % 128 < 64
-    row = lax.broadcasted_iota(jnp.int32, (8, 256), 0)
-    pick = jnp.where((row == 0) & first, 1.0, 0.0) + jnp.where((row == 1) & (~first), 1.0, 0.0)
-    squares = dot_nt(pick, prod)
+    joint_terms = three_terms(joint)
+    joint_hi, joint_lo = joint_terms[:2]
+    first = lax.broadcasted_iota(jnp.int32, (8, 128), 1) < 64
+    row = lax.broadcasted_iota(jnp.int32, (8, 128), 0)
+    pick = (jnp.where((row == 0) & first, 1.0, 0.0) + jnp.where((row == 1) & (~first), 1.0, 0.0)).astype(jnp.bfloat16)
     j = lax.broadcasted_iota(jnp.int32, (256, 128), 0)
     lane = lax.broadcasted_iota(jnp.int32, (256, 128), 1)
     own = (j // 64) % 2 == lane // 64
     dim = j % 64 + 64 * (j // 128)
-    onehot = jnp.where(own & (dim == pivots_row), 1.0, 0.0)
-    picked = dot_nn(basis, onehot)
+    onehot = jnp.where(own & (dim == pivots_row), 1.0, 0.0).astype(jnp.bfloat16)
     r = lax.broadcasted_iota(jnp.int32, (64, 128), 0)
     c = lax.broadcasted_iota(jnp.int32, (64, 128), 1)
-    weight = jnp.sum(jnp.where(c % 64 == r, picked, 0.0), axis=0, keepdims=True) * math.sqrt(128)
-    zlo, zhi = halves(za, zb)
-    proj = dot_nt(jnp.concatenate([zlo, zhi], axis=1), masked_pair(low, high)) * weight
+    diagonal = c % 64 == r
+    z_hi, z_lo = two_terms(jnp.concatenate(halves(za, zb), axis=1))
+    square = dot_full(three_terms(jnp.concatenate([lo_a, hi_a], axis=1)), joint_terms)
+    low, high = whiten(None, square[:, :128], square[:, 128:])
+    image = three_terms(jnp.concatenate([low, high], axis=1))
+    gram = dot_full(image, [masked_pair(t[:, :128], t[:, 128:]) for t in image], NT)
+    low, high = whiten(gram, low, high)
+    basis = jnp.concatenate([low, high], axis=1)
+    basis_hi, basis_lo = two_terms(basis)
+    both = jnp.concatenate([basis_hi, basis_lo], axis=0)
+    image = dot_bf16(both, joint_hi)
+    image = image[:64] + (image[64:] + dot_bf16(basis_hi, joint_lo))
+    prod = low * image[:, :128] + high * image[:, 128:]
+    prod_hi, prod_lo = two_terms(prod)
+    squares = dot_bf16(pick, prod_hi, NT) + dot_bf16(pick, prod_lo, NT)
+    picked = dot_bf16(both, onehot)
+    picked = picked[:64] + picked[64:]
+    weight = jnp.sum(jnp.where(diagonal, picked, 0.0), axis=0, keepdims=True) * math.sqrt(128)
+    pair_hi, pair_lo = masked_pair(basis_hi[:, :128], basis_hi[:, 128:]), masked_pair(basis_lo[:, :128], basis_lo[:, 128:])
+    proj = dot_bf16(jnp.concatenate([z_hi, z_lo], axis=0), pair_hi, NT)
+    proj = (proj[:32] + (proj[32:] + dot_bf16(z_hi, pair_lo, NT))) * weight
     return jnp.sqrt(squares[:2]), proj
 
 

time: 30.4 us -> 29.8 us (0.980)
  Pallas kernels: 29.7 us -> 29.1 us
    pallas_call x1, Pallas kernels: 4.48 us -> 3.89 us  [local(): pl.pallas_call(solve_kernel, out_shape=(jax.ShapeDtypeStruct((2, 64), jnp...]
where the time goes in v7:
time: 29.8 us; the launch traced here: 29.7 us
  Pallas kernels  29.1 us (98%)
  between operations  0.65 us (2%)
    pallas_call x1, Pallas kernels, sum_call(): pl.pallas_call(sum_kernel, out_shape=(jax.ShapeDtypeStruct((64, 128), f32...  25.2 us
    pallas_call x1, Pallas kernels, local(): pl.pallas_call(solve_kernel, out_shape=(jax.ShapeDtypeStruct((2, 64), jnp...  3.89 us

profile of v7, /device:TPU:7, one launch (start us, length us, event | category | flops | bytes accessed | tf_op | source)
XLA Modules:
  0.0 29.7 jit_solution(6627123617364302714)
XLA Ops:
  0.6 0.0 copy-start
  0.6 25.2 %shard_map.50 = (f32[64,128]{1,0:T(8,128)S(1)}, f32[2,128,128]{2,1,0:T(8,128)S(1)}) custom-call(bf16[64,32768]{1,0:T(8,128)(2,1)} %bitcast.2, bf16[32768,128]{1,0:T(8,128)(2,1)} %sketch_hbm.1), custom_call_target="tpu_custom_call" | custom-call | tf_op jit(solution)/shard_map/pallas_call | solution.py:298
  25.8 0.0 copy-done
  25.8 3.9 %shard_map.51 = (f32[2,64]{1,0:T(2,128)}, f32[2,32,64]{2,1,0:T(8,128)}) custom-call(f32[64,128]{1,0:T(8,128)S(1)} %get-tuple-element.6.own_ref, f32[2,128,128]{2,1,0:T(8,128)S(1)} %get-tuple-element.7.grams_ref, s32[2,64]{1,0:T(2,128)S(1)} %copy-done), custom_call_target="tpu_custom_call" | custom-call | tf_op jit(solution)/shard_map/pallas_call | solution.py:336
Async XLA Ops:
  0.6 25.2 %copy-start = (s32[2,64]{1,0:T(2,128)S(1)}, s32[2,64]{1,0:T(2,128)}, u32[]{:S(2)}) copy-start(s32[2,64]{1,0:T(2,128)} %pivots_ref.1) | copy-start | bytes 1540

commit v8 on v7

--- a/solution.py
+++ b/solution.py
@@ -206,24 +206,22 @@
     nd, nw = 16, 16
     core = lax.rem(d, 2)
     partner = d + 1 - 2 * core
-    depth = sketch.shape[1]
-    loads = []
+    depth = sketch.shape[0] // CHUNKS
     for i in range(CHUNKS):
-        a = pltpu.make_async_copy(sketch_hbm.at[pl.ds(i * depth, depth), :], sketch.at[i], in_sem.at[0, i])
-        b = pltpu.make_async_copy(snap_hbm.at[:, pl.ds(i * depth, depth)], snap.at[i], in_sem.at[1, i])
-        a.start()
-        b.start()
-        loads.append((a, b))
+        rows = pl.ds(i * depth, depth)
+        pltpu.make_async_copy(sketch_hbm.at[rows, :], sketch.at[rows, :], in_sem.at[i]).start()
+        pltpu.make_async_copy(snap_hbm.at[:, rows], snap.at[:, rows], in_sem.at[i]).start()
     gath[...] = jnp.zeros_like(gath)
     barrier = pltpu.get_barrier_semaphore()
     for k in range(1, 16):
         pl.semaphore_signal(barrier, inc=1, device_id={"dof": lax.rem(d + k, nd)}, device_id_type=MESH)
         pl.semaphore_signal(barrier, inc=1, device_id={"win": lax.rem(w + k, nw)}, device_id_type=MESH)
     total = jnp.zeros((64, 128), jnp.float32)
+    chunk_bytes = pl.ds(0, depth + depth // 2)
     for i in range(CHUNKS):
-        for copy in loads[i]:
-            copy.wait()
-        total = total + jnp.dot(snap[i], sketch[i], preferred_element_type=jnp.float32)
+        rows = pl.ds(i * depth, depth)
+        pltpu.make_async_copy(sketch_hbm.at[chunk_bytes, :], sketch.at[chunk_bytes, :], in_sem.at[i]).wait()
+        total = total + jnp.dot(snap[:, rows], sketch[rows, :], preferred_element_type=jnp.float32)
     for p in range(16):
         part[p] = total[4 * p : 4 * p + 4, :]
     pl.semaphore_wait(barrier, 30)
@@ -250,7 +248,7 @@
         dst = gath.at[w, pl.ds(first, count)]
 
         def send(v, carry):
-            rdma(src, dst, xy_send.at[v], xy_recv.at[w], {"win": v}).start()
+            rdma(src, dst, xy_send, xy_recv, {"win": v}).start()
             return carry
 
         lax.fori_loop(w + 1, 16, send, 0)
@@ -273,19 +271,24 @@
     count = jnp.full((128, 128), 64 * w, jnp.int32).astype(jnp.float32)
     inv_a, inv_b = 1.0 / (count + 32.0), 1.0 / (count + 64.0)
     own_a, own_b = eye + ma * inv_a, eye + mab * inv_b
-    for v in range(15):
-        @pl.when(v < w)
+
+    def blocks(count):
+        some = gath.at[pl.ds(0, count)]
+        return rdma(some, some, xy_send, xy_recv, {"dof": partner})
+
+    for count in range(1, 16):
+        @pl.when(w == count)
         def _():
-            rdma(gath.at[v], gath.at[v], xy_send.at[v], xy_recv.at[v], {"win": v}).wait_recv()
+            blocks(count).wait_recv()
     gram_send[...] = gram_split(gath[...].reshape(512, 128))
     swap = rdma(gram_send, gram_recv, pair_sem.at[0], pair_sem.at[1], {"dof": partner})
     swap.start()
     rdma(part.at[fifteen], rs_buf.at[fifteen], rs_send, rs_recv, {"dof": partner}).wait_send()
     rdma(ag_buf.at[fifteen], ag_buf.at[fifteen], ag_send, ag_other, {"dof": partner}).wait_send()
-    for v in range(1, 16):
-        @pl.when(v > w)
+    for count in range(1, 16):
+        @pl.when(w == 15 - count)
         def _():
-            rdma(ag_buf.at[eight], gath.at[w], xy_send.at[v], xy_recv.at[v], {"win": v}).wait_send()
+            blocks(count).wait_send()
     swap.wait()
     base = gram_send[...] + gram_recv[...]
     grams_ref[0] = own_a + base * inv_a
@@ -301,22 +304,22 @@
         in_specs=[pl.BlockSpec(memory_space=pl.ANY)] * 2,
         out_specs=(pl.BlockSpec(memory_space=pltpu.VMEM),) * 2,
         scratch_shapes=[
-            pltpu.VMEM((CHUNKS, 64, depth), jnp.bfloat16),
-            pltpu.VMEM((CHUNKS, depth, 128), jnp.bfloat16),
+            pltpu.VMEM((64, CHUNKS * depth), jnp.bfloat16),
+            pltpu.VMEM((CHUNKS * depth, 128), jnp.bfloat16),
             pltpu.VMEM((16, 4, 128), f32),
             pltpu.VMEM((16, 4, 128), f32),
             pltpu.VMEM((16, 4, 128), f32),
             pltpu.VMEM((16, 8, 4, 128), f32),
             pltpu.VMEM((128, 128), f32),
             pltpu.VMEM((128, 128), f32),
-            pltpu.SemaphoreType.DMA((2, CHUNKS)),
+            pltpu.SemaphoreType.DMA((CHUNKS,)),
             pltpu.SemaphoreType.DMA,
             pltpu.SemaphoreType.DMA,
             pltpu.SemaphoreType.DMA,
             pltpu.SemaphoreType.DMA((8,)),
             pltpu.SemaphoreType.DMA,
-            pltpu.SemaphoreType.DMA((16,)),
-            pltpu.SemaphoreType.DMA((16,)),
+            pltpu.SemaphoreType.DMA,
+            pltpu.SemaphoreType.DMA,
             pltpu.SemaphoreType.DMA((2,)),
         ],
         compiler_params=pltpu.CompilerParams(collective_id=0, has_side_effects=True, vmem_limit_bytes=52 * 1024 * 1024),

time: 29.8 us -> 29.5 us (0.990)
  Pallas kernels: 29.1 us -> 28.7 us
    pallas_call x1, Pallas kernels: 25.2 us -> 24.8 us  [sum_call(): pl.pallas_call(sum_kernel, out_shape=(jax.ShapeDtypeStruct((64, 128), f32...]
where the time goes in v8:
time: 29.5 us; the launch traced here: 29.4 us
  Pallas kernels  28.7 us (97%)
  between operations  0.65 us (2%)
    pallas_call x1, Pallas kernels, sum_call(): pl.pallas_call(sum_kernel, out_shape=(jax.ShapeDtypeStruct((64, 128), f32...  24.8 us
    pallas_call x1, Pallas kernels, local(): pl.pallas_call(solve_kernel, out_shape=(jax.ShapeDtypeStruct((2, 64), jnp...  3.89 us

profile of v8, /device:TPU:7, one launch (start us, length us, event | category | flops | bytes accessed | tf_op | source)
XLA Modules:
  0.0 29.4 jit_solution(10598173679113321453)
XLA Ops:
  0.6 0.0 copy-start
  0.6 24.8 %shard_map.50 = (f32[64,128]{1,0:T(8,128)S(1)}, f32[2,128,128]{2,1,0:T(8,128)S(1)}) custom-call(bf16[64,32768]{1,0:T(8,128)(2,1)} %bitcast.2, bf16[32768,128]{1,0:T(8,128)(2,1)} %sketch_hbm.1), custom_call_target="tpu_custom_call" | custom-call | tf_op jit(solution)/shard_map/pallas_call | solution.py:301
  25.5 0.0 copy-done
  25.5 3.9 %shard_map.51 = (f32[2,64]{1,0:T(2,128)}, f32[2,32,64]{2,1,0:T(8,128)}) custom-call(f32[64,128]{1,0:T(8,128)S(1)} %get-tuple-element.6.own_ref, f32[2,128,128]{2,1,0:T(8,128)S(1)} %get-tuple-element.7.grams_ref, s32[2,64]{1,0:T(2,128)S(1)} %copy-done), custom_call_target="tpu_custom_call" | custom-call | tf_op jit(solution)/shard_map/pallas_call | solution.py:339
Async XLA Ops:
  0.6 24.8 %copy-start = (s32[2,64]{1,0:T(2,128)S(1)}, s32[2,64]{1,0:T(2,128)}, u32[]{:S(2)}) copy-start(s32[2,64]{1,0:T(2,128)} %pivots_ref.1) | copy-start | bytes 1540

commit v9 on v8

--- a/solution.py
+++ b/solution.py
@@ -117,24 +117,18 @@
 
 def solve_windows(pa, pb, za, zb, pivots_row):
     alo, ahi = halves(pa, pb)
-    zero = jnp.zeros((64, 64), jnp.float32)
-
-    def block_rows(x, first):
-        left = jnp.concatenate([x[:, :64], zero] if first else [zero, x[:, 64:]], axis=1)
-        return left
-
-    lo_a, lo_b = alo[:64], alo[64:]
-    hi_a, hi_b = ahi[:64], ahi[64:]
-    joint = jnp.concatenate(
-        [
-            jnp.concatenate([block_rows(lo_a, True), block_rows(hi_a, True)], axis=1),
-            jnp.concatenate([block_rows(lo_a, False), block_rows(hi_a, False)], axis=1),
-            jnp.concatenate([block_rows(lo_b, True), block_rows(hi_b, True)], axis=1),
-            jnp.concatenate([block_rows(lo_b, False), block_rows(hi_b, False)], axis=1),
-        ],
-        axis=0,
-    )
-    joint_terms = three_terms(joint)
+    wide = jnp.concatenate([alo, ahi], axis=1)
+    of_a = lax.broadcasted_iota(jnp.int32, (64, 256), 1) % 128 < 64
+
+    def spread_rows(x):
+        zero = jnp.zeros((64, 256), x.dtype)
+        return jnp.concatenate(
+            [jnp.where(of_a, x[:64], zero), jnp.where(of_a, zero, x[:64]), jnp.where(of_a, x[64:], zero), jnp.where(of_a, zero, x[64:])],
+            axis=0,
+        )
+
+    wide_terms = three_terms(wide)
+    joint_terms = [spread_rows(t) for t in wide_terms]
     joint_hi, joint_lo = joint_terms[:2]
     first = lax.broadcasted_iota(jnp.int32, (8, 128), 1) < 64
     row = lax.broadcasted_iota(jnp.int32, (8, 128), 0)
@@ -148,7 +142,7 @@
     c = lax.broadcasted_iota(jnp.int32, (64, 128), 1)
     diagonal = c % 64 == r
     z_hi, z_lo = two_terms(jnp.concatenate(halves(za, zb), axis=1))
-    square = dot_full(three_terms(jnp.concatenate([lo_a, hi_a], axis=1)), joint_terms)
+    square = dot_full([t[:64] for t in wide_terms], joint_terms)
     low, high = whiten(None, square[:, :128], square[:, 128:])
     image = three_terms(jnp.concatenate([low, high], axis=1))
     gram = dot_full(image, [masked_pair(t[:, :128], t[:, 128:]) for t in image], NT)

time: 29.5 us -> 29.4 us (level)
  no operation moved by 1% of the time
where the time goes in v9:
time: 29.4 us
  Pallas kernels  28.7 us (98%)
  between operations  0.65 us (2%)
    pallas_call x1, Pallas kernels, sum_call(): pl.pallas_call(sum_kernel, out_shape=(jax.ShapeDtypeStruct((64, 128), f32...  24.8 us
    pallas_call x1, Pallas kernels, local(): pl.pallas_call(solve_kernel, out_shape=(jax.ShapeDtypeStruct((2, 64), jnp...  3.88 us

profile of v9, /device:TPU:7, one launch (start us, length us, event | category | flops | bytes accessed | tf_op | source)
XLA Modules:
  0.0 29.4 jit_solution(17233808100805024470)
XLA Ops:
  0.6 0.0 copy-start
  0.6 24.8 %shard_map.50 = (f32[64,128]{1,0:T(8,128)S(1)}, f32[2,128,128]{2,1,0:T(8,128)S(1)}) custom-call(bf16[64,32768]{1,0:T(8,128)(2,1)} %bitcast.2, bf16[32768,128]{1,0:T(8,128)(2,1)} %sketch_hbm.1), custom_call_target="tpu_custom_call" | custom-call | tf_op jit(solution)/shard_map/pallas_call | solution.py:295
  25.5 0.0 copy-done
  25.5 3.9 %shard_map.51 = (f32[2,64]{1,0:T(2,128)}, f32[2,32,64]{2,1,0:T(8,128)}) custom-call(f32[64,128]{1,0:T(8,128)S(1)} %get-tuple-element.6.own_ref, f32[2,128,128]{2,1,0:T(8,128)S(1)} %get-tuple-element.7.grams_ref, s32[2,64]{1,0:T(2,128)S(1)} %copy-done), custom_call_target="tpu_custom_call" | custom-call | tf_op jit(solution)/shard_map/pallas_call | solution.py:333
Async XLA Ops:
  0.6 24.8 %copy-start = (s32[2,64]{1,0:T(2,128)S(1)}, s32[2,64]{1,0:T(2,128)}, u32[]{:S(2)}) copy-start(s32[2,64]{1,0:T(2,128)} %pivots_ref.1) | copy-start | bytes 1540

commit v10 on v9

--- a/solution.py
+++ b/solution.py
@@ -69,10 +69,10 @@
         return jnp.broadcast_to(x[p : p + 1, :], (8, 128))
 
     for kb in range(8):
-        cols = []
-        for j in range(8):
-            idx = base + (8 * kb + j)
-            cols.append({i: jnp.take_along_axis(pivots_from[i], idx, axis=1) for i in range(kb, 8)})
+        cols = [{} for _ in range(8)]
+        for i in range(kb, 8):
+            for j in range(8):
+                cols[j][i] = jnp.take_along_axis(pivots_from[i], base + (8 * kb + j), axis=1)
         diag = None
         for p in range(0, 8, 2):
             q = p + 1

time: 29.4 us -> 29.4 us (level)
  no operation moved by 1% of the time
where the time goes in v10:
time: 29.4 us
  Pallas kernels  28.7 us (98%)
  between operations  0.65 us (2%)
    pallas_call x1, Pallas kernels, sum_call(): pl.pallas_call(sum_kernel, out_shape=(jax.ShapeDtypeStruct((64, 128), f32...  24.8 us
    pallas_call x1, Pallas kernels, local(): pl.pallas_call(solve_kernel, out_shape=(jax.ShapeDtypeStruct((2, 64), jnp...  3.88 us

profile of v10, /device:TPU:7, one launch (start us, length us, event | category | flops | bytes accessed | tf_op | source)
XLA Modules:
  0.0 29.4 jit_solution(17233808100805024470)
XLA Ops:
  0.6 0.0 copy-start
  0.6 24.8 %shard_map.50 = (f32[64,128]{1,0:T(8,128)S(1)}, f32[2,128,128]{2,1,0:T(8,128)S(1)}) custom-call(bf16[64,32768]{1,0:T(8,128)(2,1)} %bitcast.2, bf16[32768,128]{1,0:T(8,128)(2,1)} %sketch_hbm.1), custom_call_target="tpu_custom_call" | custom-call | tf_op jit(solution)/shard_map/pallas_call | solution.py:295
  25.5 0.0 copy-done
  25.5 3.9 %shard_map.51 = (f32[2,64]{1,0:T(2,128)}, f32[2,32,64]{2,1,0:T(8,128)}) custom-call(f32[64,128]{1,0:T(8,128)S(1)} %get-tuple-element.6.own_ref, f32[2,128,128]{2,1,0:T(8,128)S(1)} %get-tuple-element.7.grams_ref, s32[2,64]{1,0:T(2,128)S(1)} %copy-done), custom_call_target="tpu_custom_call" | custom-call | tf_op jit(solution)/shard_map/pallas_call | solution.py:333
Async XLA Ops:
  0.6 24.8 %copy-start = (s32[2,64]{1,0:T(2,128)S(1)}, s32[2,64]{1,0:T(2,128)}, u32[]{:S(2)}) copy-start(s32[2,64]{1,0:T(2,128)} %pivots_ref.1) | copy-start | bytes 1540
